TPU v7x, 32 devices: a whole 2x2x4 slice. The times are simulated.
32 devices in a mesh: blk: 8 (over z, y), off: 4 (over x, core).
Axes of the slice: x: 2, y: 2, z: 4, core: 2. Of those that a mesh axis runs over, the one named last changes fastest.
Arguments:
- orbitals: bfloat16 [8, 48, 2304], P('blk'), may hold values from -1.5 to 1.5
Outputs:
- exchange: float32 [8, 48, 2304], P('blk', 'off')
All inputs are finite; a program needn't handle non-finite values.
Results may differ from a plain program's by a relative error of at most 0.00055.
Values may be sent and summed in bfloat16 or wider, within the bound.
No kernel may reach another device: no remote copies, remote signals or barrier semaphores. Data moves between devices by JAX's collectives and lax.ppermute only.
A program may use at most 64 MiB of HBM per device.

v0:
```python
import math

import jax
import jax.numpy as jnp
from jax import lax
from jax.sharding import PartitionSpec as P

cell_edge = 59.0
screen_rate = 0.106


def from_behind(block, axis, distance):
    devices = range(lax.axis_size(axis))
    route = [((i - distance) % len(devices), i) for i in devices]
    return lax.ppermute(block, axis, route)


def screened_kernel(grid_edge):
    points = jnp.arange(grid_edge, dtype=jnp.int32)
    signed = jnp.where(points > grid_edge // 2, points - grid_edge, points)
    half_points = jnp.arange(grid_edge // 2 + 1, dtype=jnp.int32)
    squared = (
        signed[:, None, None] ** 2 + signed[None, :, None] ** 2 + half_points[None, None, :] ** 2
    )
    wave_sq = squared.astype(jnp.float32) * jnp.float32((2.0 * math.pi / cell_edge) ** 2)
    safe_sq = jnp.where(squared == 0, jnp.float32(1.0), wave_sq)
    screened = 4.0 * math.pi * -jnp.expm1(-safe_sq / (4.0 * screen_rate**2)) / safe_sq
    return jnp.where(squared == 0, jnp.float32(math.pi / screen_rate**2), screened)


def dft_tables(grid_edge):
    points = jnp.arange(grid_edge, dtype=jnp.int32)
    phase = points[:, None] * points[None, :] % grid_edge
    angles = phase.astype(jnp.float32) * jnp.float32(2.0 * math.pi / grid_edge)
    cosine = jnp.cos(angles)
    sine = jnp.sin(angles)
    half_size = grid_edge // 2 + 1
    half_points = points[:half_size]
    weights = jnp.where((half_points == 0) | (half_points == grid_edge // 2), 1.0, 2.0).astype(
        jnp.float32
    )
    weights = weights / jnp.float32(grid_edge**3)
    cos_half = cosine[:, :half_size]
    sin_half = sine[:, :half_size]
    first_table = jnp.stack([cos_half, -sin_half], axis=1)
    forward = jnp.stack([jnp.stack([cosine, -sine]), jnp.stack([sine, cosine])]).transpose(
        0, 2, 1, 3
    )
    backward = jnp.stack([jnp.stack([cosine, sine]), jnp.stack([-sine, cosine])]).transpose(
        0, 2, 1, 3
    )
    back_cos = (cos_half * weights[None, :]).T
    back_sin = (sin_half * weights[None, :]).T
    last_table = jnp.stack([back_cos, -back_sin])
    return (first_table, forward, backward, last_table)


def contract(form, data, table):
    return jnp.einsum(form, data, table, precision=lax.Precision.HIGHEST)


def potential(density, tables, kernel):
    first_table, forward, backward, last_table = tables
    spectrum = contract("pxyz,zck->cpxyk", density, first_table)
    spectrum = contract("cpxyk,cydv->dpxvk", spectrum, forward)
    spectrum = contract("dpxvk,dxeu->epuvk", spectrum, forward)
    spectrum = spectrum * kernel
    spectrum = contract("epuvk,eufx->fpxvk", spectrum, backward)
    spectrum = contract("fpxvk,fvgy->gpxyk", spectrum, backward)
    return contract("gpxyk,gkz->pxyz", spectrum, last_table)


def pair_terms(left_block, right_block, tables, kernel):
    band_count, grid_edge, plane_size = left_block.shape
    right_fields = right_block.astype(jnp.float32)
    right_cubes = right_fields.reshape(band_count, grid_edge, grid_edge, grid_edge)
    home_terms = jnp.zeros(left_block.shape, jnp.float32)
    other_terms = jnp.zeros(left_block.shape, jnp.float32)

    def step(first_band, carry):
        home_acc, other_acc = carry
        left_band = lax.dynamic_index_in_dim(left_block, first_band, 0, keepdims=False).astype(
            jnp.float32
        )
        densities = left_band.reshape(1, grid_edge, grid_edge, grid_edge) * right_cubes
        fields = potential(densities, tables, kernel).reshape(band_count, grid_edge, plane_size)
        home_row = jnp.sum(right_fields * fields, axis=0)
        home_acc = lax.dynamic_update_index_in_dim(home_acc, home_row, first_band, 0)
        return (home_acc, other_acc)

    return lax.fori_loop(0, band_count, step, (home_terms, other_terms))


def on_device(orbitals):
    band_count, grid_edge, plane_size = orbitals.shape
    cycle_size = lax.axis_size("blk")
    digit_count = cycle_size.bit_length() - 1
    offset_group = lax.axis_index("off")
    distance = jnp.where(offset_group == 0, cycle_size // 2, offset_group)
    tables = dft_tables(grid_edge)
    kernel = screened_kernel(grid_edge)
    ahead = orbitals
    for bit_level in range(digit_count):
        arrived = from_behind(ahead, "blk", -(1 << bit_level))
        ahead = jnp.where((distance >> bit_level) % 2 == 1, arrived, ahead)
    behind = orbitals
    for bit_level in range(digit_count):
        arrived = from_behind(behind, "blk", 1 << bit_level)
        behind = jnp.where((distance >> bit_level) % 2 == 1, arrived, behind)
    behind = jnp.where(offset_group == 0, orbitals, behind)
    ahead_terms, unused_ahead = pair_terms(orbitals, ahead, tables, kernel)
    behind_terms, unused_behind = pair_terms(orbitals, behind, tables, kernel)
    summed = ahead_terms + behind_terms
    summed = jnp.float32(-0.25) * summed
    return lax.psum_scatter(summed, "off", scatter_dimension=1, tiled=True)


def solution(mesh):
    return jax.shard_map(
        on_device,
        mesh=mesh,
        in_specs=(P("blk", None, None),),
        out_specs=P("blk", "off", None),
        check_vma=False,
    )
```

profile of v0, /device:TPU:0, one launch (start us, length us, event | category | flops | bytes accessed | tf_op | source)
XLA Modules:
  0.0 179.9 jit_solution(9857174950429761413)
XLA Ops:
  6.5 1.3 copy.32
  7.9 6.1 %collective-permute-start = (bf16[1,48,2304]{2,0,1:T(2,128)(2,1)S(1)}, bf16[1,48,2304]{2,0,1:T(2,128)(2,1)S(1)}, u32[]{:S(2)}, u32[]{:S(2)}) collective-permute-start(bf16[1,48,2304]{2,0,1:T(2,128)(2,1)S(1)} %copy.32), channel_id=1, source_target_pairs={{4,0},{8,4},{12,8},{16,12},{20,16},{24,20},{28,24},{0,28},{5,1},{9... | collective-permute-start | bytes 663560 | tf_op jit(solution)/shard_map/ppermute | solution.py:15
  14.9 15.7 %collective-permute-done = bf16[1,48,2304]{2,0,1:T(2,128)(2,1)S(1)} collective-permute-done((bf16[1,48,2304]{2,0,1:T(2,128)(2,1)S(1)}, bf16[1,48,2304]{2,0,1:T(2,128)(2,1)S(1)}, u32[]{:S(2)}, u32[]{:S(2)}) %collective-permute-start) | collective-permute-done | bytes 221216 | tf_op jit(solution)/shard_map/ppermute | solution.py:15
  30.7 1.1 broadcast_select_fusion.1
  31.8 1.7 collective-permute-start.4
  33.6 2.3 %collective-permute-start.1 = (bf16[1,48,2304]{2,0,1:T(2,128)(2,1)S(1)}, bf16[1,48,2304]{2,0,1:T(2,128)(2,1)S(1)}, u32[]{:S(2)}, u32[]{:S(2)}) collective-permute-start(bf16[1,48,2304]{2,0,1:T(2,128)(2,1)S(1)} %get-tuple-element.50), channel_id=1, source_target_pairs={{8,0},{12,4},{16,8},{20,12},{24,16},{28,20},{0,24},{4,28},{9,1},{1... | collective-permute-start | bytes 663560 | tf_op jit(solution)/shard_map/ppermute | solution.py:15
  35.9 10.9 %collective-permute-done.4 = bf16[1,48,2304]{2,0,1:T(2,128)(2,1)S(1)} collective-permute-done((bf16[1,48,2304]{2,0,1:T(2,128)(2,1)S(1)}, bf16[1,48,2304]{2,0,1:T(2,128)(2,1)S(1)}, u32[]{:S(2)}, u32[]{:S(2)}) %collective-permute-start.4) | collective-permute-done | bytes 221216 | tf_op jit(solution)/shard_map/ppermute | solution.py:15
  47.5 17.9 %collective-permute-start.5 = (bf16[1,48,2304]{2,0,1:T(2,128)(2,1)S(1)}, bf16[1,48,2304]{2,0,1:T(2,128)(2,1)S(1)}, u32[]{:S(2)}, u32[]{:S(2)}) collective-permute-start(bf16[1,48,2304]{2,0,1:T(2,128)(2,1)S(1)} %broadcast_select_fusion.3), channel_id=1, source_target_pairs={{16,0},{20,4},{24,8},{28,12},{0,16},{4,20},{8,24},{12,28},{17,1},{... | collective-permute-start | bytes 663560 | tf_op jit(solution)/shard_map/ppermute | solution.py:15
  66.2 17.6 %collective-permute-done.5 = bf16[1,48,2304]{2,0,1:T(2,128)(2,1)S(1)} collective-permute-done((bf16[1,48,2304]{2,0,1:T(2,128)(2,1)S(1)}, bf16[1,48,2304]{2,0,1:T(2,128)(2,1)S(1)}, u32[]{:S(2)}, u32[]{:S(2)}) %collective-permute-start.5) | collective-permute-done | bytes 221216 | tf_op jit(solution)/shard_map/ppermute | solution.py:15
  83.8 9.0 %collective-permute-done.2 = bf16[1,48,2304]{2,0,1:T(2,128)(2,1)S(1)} collective-permute-done((bf16[1,48,2304]{2,0,1:T(2,128)(2,1)S(1)}, bf16[1,48,2304]{2,0,1:T(2,128)(2,1)S(1)}, u32[]{:S(2)}, u32[]{:S(2)}) %collective-permute-start.2) | collective-permute-done | bytes 221216 | tf_op jit(solution)/shard_map/ppermute | solution.py:15
  92.9 4.1 %multiply_reduce_fusion.1 = (f32[48,2304]{1,0:T(8,128)S(1)}, f32[48,2304]{1,0:T(8,128)}) fusion(bf16[1,48,2304]{2,0,1:T(2,128)(2,1)S(1)} %collective-permute-done.2, bf16[1,48,2304]{2,0,1:T(2,128)(2,1)S(1)} %broadcast_select_fusion.4, pred[]{:T(512)S(6)} %eq.46, bf16[1,48,2304]{2,1,0:T(8,128)(2,1)S(1)} %copy-done.4, ...), kind=kLoop, calls=%fused_computation.44 | loop fusion | flops 884736 | bytes 1990658 | tf_op jit(solution)/shard_map/while/body/eval_jaxpr/mul | solution.py:85
  97.0 0.7 reshape.233
  97.7 4.2 %convolution_bitcast_fusion.1 = f32[2,48,48,25]{2,3,1,0:T(8,128)S(1)} fusion(f32[48,48,48,1]{2,1,0,3:T(8,128)S(1)} %reshape.233, f32[48,1,25]{0,2,1:T(8,128)S(1)} %get-tuple-element.70, f32[48,1,25]{0,2,1:T(8,128)S(1)} %get-tuple-element.71), kind=kOutput, calls=%fused_computation.1 | convolution fusion | flops 66357600 | bytes 912768 | tf_op jit(solution)/shard_map/while/body/eval_jaxpr/pxyz,zck->cpxyk/dot_general | solution.py:59
  102.0 2.8 %convolution_bitcast_fusion.9 = f32[2,48,48,25,1]{1,2,3,0,4:T(8,128)S(1)} fusion(f32[2,48,48,25]{2,3,1,0:T(8,128)S(1)} %convolution_bitcast_fusion.1, f32[1,2,48,48]{2,3,0,1:T(8,128)S(1)} %get-tuple-element.54, f32[1,2,48,48]{2,3,0,1:T(8,128)S(1)} %get-tuple-element.72), kind=kOutput, calls=%fused_computation.9 | convolution fusion | flops 132719616 | bytes 958464 | tf_op jit(solution)/shard_map/while/body/eval_jaxpr/cpxyk,cydv->dpxvk/dot_general | solution.py:59
  104.7 2.5 %fusion.1 = f32[2,48,48,25,1]{2,1,3,0,4:T(8,128)S(1)} fusion(f32[2,48,48,25,1]{1,2,3,0,4:T(8,128)S(1)} %convolution_bitcast_fusion.9, f32[48,48,25]{1,0,2:T(8,128)S(1)} %fusion.10, f32[1,2,48,48]{2,3,0,1:T(8,128)S(1)} %get-tuple-element.54, f32[1,2,48,48]{2,3,0,1:T(8,128)S(1)} %get-tuple-element.72), kind=kOutput, calls=%fused_computation.13 | convolution fusion | flops 132834816 | bytes 1188864 | tf_op jit(solution)/shard_map/while/body/eval_jaxpr/dpxvk,dxeu->epuvk/dot_general | solution.py:59
  107.3 1.2 convolution_bitcast_fusion.8
  108.5 2.1 %convolution_bitcast_fusion.7 = f32[2,48,48,25]{1,2,3,0:T(8,128)S(1)} fusion(f32[2,48,48,25,1]{2,1,0,3,4:T(8,128)S(1)} %convolution_bitcast_fusion.8, f32[2,48,2,48,1]{1,3,2,0,4:T(8,128)S(1)} %get-tuple-element.51), kind=kOutput, calls=%fused_computation.7 | convolution fusion | flops 132710400 | bytes 958464 | tf_op jit(solution)/shard_map/while/body/eval_jaxpr/fpxvk,fvgy->gpxyk/dot_general | solution.py:59
  110.6 1.4 copy.41
  112.0 2.6 %convolution_bitcast_fusion.11 = f32[48,48,48]{2,1,0:T(8,128)S(1)} fusion(f32[2,48,48,25]{2,3,0,1:T(8,128)S(1)} %copy.41, f32[1,25,48]{2,1,0:T(8,128)S(1)} %get-tuple-element.69, f32[1,25,48]{2,1,0:T(8,128)S(1)} %get-tuple-element.68), kind=kOutput, calls=%fused_computation.11 | convolution fusion | flops 66357600 | bytes 912768 | tf_op jit(solution)/shard_map/while/body/eval_jaxpr/gpxyk,gkz->pxyz/dot_general | solution.py:59
  114.7 1.9 %reshape.260 = f32[1,48,2304]{2,0,1:T(1,128)} reshape(f32[48,48,48]{2,1,0:T(8,128)S(1)} %convolution_bitcast_fusion.11) | data formatting | bytes 884736 | tf_op jit(solution)/shard_map/while/body/eval_jaxpr/reshape | solution.py:86
  116.6 1.7 reshape.247
  118.4 4.2 %convolution_bitcast_fusion = f32[2,48,48,25]{2,3,1,0:T(8,128)S(1)} fusion(f32[48,48,48,1]{2,1,0,3:T(8,128)S(1)} %reshape.247, f32[48,1,25]{0,2,1:T(8,128)S(1)} %copy-done.14, f32[48,1,25]{0,2,1:T(8,128)S(1)} %copy-done.16), kind=kOutput, calls=%fused_computation | convolution fusion | flops 66357600 | bytes 912768 | tf_op jit(solution)/shard_map/while/body/eval_jaxpr/pxyz,zck->cpxyk/dot_general | solution.py:59
  122.6 2.9 %convolution_bitcast_fusion.6 = f32[2,48,48,25,1]{1,2,3,0,4:T(8,128)S(1)} fusion(f32[2,48,48,25]{2,3,1,0:T(8,128)S(1)} %convolution_bitcast_fusion, f32[1,2,48,48]{2,3,0,1:T(8,128)S(1)} %get-tuple-element.54, f32[1,2,48,48]{2,3,0,1:T(8,128)S(1)} %get-tuple-element.72), kind=kOutput, calls=%fused_computation.6 | convolution fusion | flops 132719616 | bytes 958464 | tf_op jit(solution)/shard_map/while/body/eval_jaxpr/cpxyk,cydv->dpxvk/dot_general | solution.py:59
  125.6 2.1 %fusion.3 = f32[2,48,48,25,1]{2,1,3,0,4:T(8,128)S(1)} fusion(f32[2,48,48,25,1]{1,2,3,0,4:T(8,128)S(1)} %convolution_bitcast_fusion.6, f32[48,48,25]{1,0,2:T(8,128)S(1)} %fusion.10, f32[1,2,48,48]{2,3,0,1:T(8,128)S(1)} %get-tuple-element.54, f32[1,2,48,48]{2,3,0,1:T(8,128)S(1)} %get-tuple-element.72), kind=kOutput, calls=%fused_computation.15 | convolution fusion | flops 132834816 | bytes 1188864 | tf_op jit(solution)/shard_map/while/body/eval_jaxpr/dpxvk,dxeu->epuvk/dot_general | solution.py:59
  127.7 1.2 convolution_bitcast_fusion.5
  128.9 2.1 %convolution_bitcast_fusion.4 = f32[2,48,48,25]{1,2,3,0:T(8,128)S(1)} fusion(f32[2,48,48,25,1]{2,1,0,3,4:T(8,128)S(1)} %convolution_bitcast_fusion.5, f32[2,48,2,48,1]{1,3,2,0,4:T(8,128)S(1)} %copy-done.10), kind=kOutput, calls=%fused_computation.4 | convolution fusion | flops 132710400 | bytes 958464 | tf_op jit(solution)/shard_map/while/body/eval_jaxpr/fpxvk,fvgy->gpxyk/dot_general | solution.py:59
  131.1 1.4 copy.51
  132.4 2.6 %convolution_bitcast_fusion.10 = f32[48,48,48]{2,1,0:T(8,128)S(1)} fusion(f32[2,48,48,25]{2,3,0,1:T(8,128)S(1)} %copy.51, f32[1,25,48]{2,1,0:T(8,128)S(1)} %get-tuple-element.69, f32[1,25,48]{2,1,0:T(8,128)S(1)} %get-tuple-element.68), kind=kOutput, calls=%fused_computation.10 | convolution fusion | flops 66357600 | bytes 912768 | tf_op jit(solution)/shard_map/while/body/eval_jaxpr/gpxyk,gkz->pxyz/dot_general | solution.py:59
  135.1 1.2 reshape.262
  136.4 3.6 %add_multiply_fusion = f32[1,48,2304]{2,0,1:T(1,128)} fusion(f32[1,48,2304]{2,0,1:T(1,128)S(1)} %reshape.262, f32[1,48,2304]{2,0,1:T(1,128)S(1)} %copy-done.6, bf16[1,48,2304]{2,0,1:T(2,128)(2,1)} %copy-done.8, bf16[1,48,2304]{2,0,1:T(2,128)(2,1)S(1)} %copy-done.3, pred[]{:T(512)S(6)} %eq.46, bf16[1,48,2304]{2,0,1:T(2,128)(2,1)} %copy-done.7, ...), kind=kLoop, calls=%fused_computation.42 | loop fusion | flops 995328 | bytes 2433026 | tf_op jit(solution)/shard_map/mul | solution.py:114
  141.3 30.0 %all-reduce.3.cloned.1.call-done = f32[1,48,2304]{2,0,1:T(1,128)} async-done(((f32[1,48,2304]{2,0,1:T(1,128)}), f32[1,48,2304]{2,0,1:T(1,128)}) %all-reduce.3.cloned.1.call-update) | async-done | bytes 442384
  171.3 1.6 constant_dynamic-slice_fusion
  (57 shorter events, 3.3 us)
Async XLA Ops:
  6.5 24.2 %copy-start.4 = (bf16[1,48,2304]{2,1,0:T(8,128)(2,1)S(1)}, bf16[1,48,2304]{2,1,0:T(8,128)(2,1)}, u32[]{:S(2)}) copy-start(bf16[1,48,2304]{2,1,0:T(8,128)(2,1)} %param.1) | copy-start | bytes 663556
  6.5 164.8 %all-reduce.3.cloned.1.call-start = ((), (), s32[]{:S(2)}) async-start(), calls=%async_computation | async-start | bytes 884736
  7.9 22.7 %collective-permute-start = (bf16[1,48,2304]{2,0,1:T(2,128)(2,1)S(1)}, bf16[1,48,2304]{2,0,1:T(2,128)(2,1)S(1)}, u32[]{:S(2)}, u32[]{:S(2)}) collective-permute-start(bf16[1,48,2304]{2,0,1:T(2,128)(2,1)S(1)} %copy.32), channel_id=1, source_target_pairs={{4,0},{8,4},{12,8},{16,12},{20,16},{24,20},{28,24},{0,28},{5,1},{9... | collective-permute-start | bytes 663560 | tf_op jit(solution)/shard_map/ppermute | solution.py:15
  14.0 16.8 %collective-permute-start.3 = (bf16[1,48,2304]{2,0,1:T(2,128)(2,1)S(1)}, bf16[1,48,2304]{2,0,1:T(2,128)(2,1)S(1)}, u32[]{:S(2)}, u32[]{:S(2)}) collective-permute-start(bf16[1,48,2304]{2,0,1:T(2,128)(2,1)S(1)} %copy.32), channel_id=1, source_target_pairs={{28,0},{0,4},{4,8},{8,12},{12,16},{16,20},{20,24},{24,28},{29,1},{... | collective-permute-start | bytes 663560 | tf_op jit(solution)/shard_map/ppermute | solution.py:15
  14.4 92.9 %copy-start.11 = (f32[2,48,2,48]{1,3,2,0:T(8,128)}, f32[2,48,2,48]{1,3,2,0:T(8,128)S(1)}, u32[]{:S(2)}) copy-start(f32[2,48,2,48]{1,3,2,0:T(8,128)S(1)} %get-tuple-element.52) | copy-start | bytes 110596
  14.4 94.1 %copy-start.9 = (f32[2,48,2,48,1]{1,3,2,0,4:T(8,128)}, f32[2,48,2,48,1]{1,3,2,0,4:T(8,128)S(1)}, u32[]{:S(2)}) copy-start(f32[2,48,2,48,1]{1,3,2,0,4:T(8,128)S(1)} %get-tuple-element.51) | copy-start | bytes 110596
  31.8 14.9 %collective-permute-start.4 = (bf16[1,48,2304]{2,0,1:T(2,128)(2,1)S(1)}, bf16[1,48,2304]{2,0,1:T(2,128)(2,1)S(1)}, u32[]{:S(2)}, u32[]{:S(2)}) collective-permute-start(bf16[1,48,2304]{2,0,1:T(2,128)(2,1)S(1)} %get-tuple-element.49), channel_id=1, source_target_pairs={{24,0},{28,4},{0,8},{4,12},{8,16},{12,20},{16,24},{20,28},{25,1},{... | collective-permute-start | bytes 663560 | tf_op jit(solution)/shard_map/ppermute | solution.py:15
  33.6 31.8 %collective-permute-start.1 = (bf16[1,48,2304]{2,0,1:T(2,128)(2,1)S(1)}, bf16[1,48,2304]{2,0,1:T(2,128)(2,1)S(1)}, u32[]{:S(2)}, u32[]{:S(2)}) collective-permute-start(bf16[1,48,2304]{2,0,1:T(2,128)(2,1)S(1)} %get-tuple-element.50), channel_id=1, source_target_pairs={{8,0},{12,4},{16,8},{20,12},{24,16},{28,20},{0,24},{4,28},{9,1},{1... | collective-permute-start | bytes 663560 | tf_op jit(solution)/shard_map/ppermute | solution.py:15
  47.5 49.5 %copy-start = (bf16[1,48,2304]{2,0,1:T(2,128)(2,1)}, bf16[1,48,2304]{2,0,1:T(2,128)(2,1)S(1)}, u32[]{:S(2)}) copy-start(bf16[1,48,2304]{2,0,1:T(2,128)(2,1)S(1)} %broadcast_select_fusion.3) | copy-start | bytes 663556
  47.5 36.4 %collective-permute-start.5 = (bf16[1,48,2304]{2,0,1:T(2,128)(2,1)S(1)}, bf16[1,48,2304]{2,0,1:T(2,128)(2,1)S(1)}, u32[]{:S(2)}, u32[]{:S(2)}) collective-permute-start(bf16[1,48,2304]{2,0,1:T(2,128)(2,1)S(1)} %broadcast_select_fusion.3), channel_id=1, source_target_pairs={{16,0},{20,4},{24,8},{28,12},{0,16},{4,20},{8,24},{12,28},{17,1},{... | collective-permute-start | bytes 663560 | tf_op jit(solution)/shard_map/ppermute | solution.py:15
  66.0 30.9 %copy-start.2 = (bf16[1,48,2304]{2,0,1:T(2,128)(2,1)}, bf16[1,48,2304]{2,0,1:T(2,128)(2,1)S(1)}, u32[]{:S(2)}) copy-start(bf16[1,48,2304]{2,0,1:T(2,128)(2,1)S(1)} %broadcast_select_fusion.4) | copy-start | bytes 663556
  66.0 26.8 %collective-permute-start.2 = (bf16[1,48,2304]{2,0,1:T(2,128)(2,1)S(1)}, bf16[1,48,2304]{2,0,1:T(2,128)(2,1)S(1)}, u32[]{:S(2)}, u32[]{:S(2)}) collective-permute-start(bf16[1,48,2304]{2,0,1:T(2,128)(2,1)S(1)} %broadcast_select_fusion.4), channel_id=1, source_target_pairs={{16,0},{20,4},{24,8},{28,12},{0,16},{4,20},{8,24},{12,28},{17,1},{... | collective-permute-start | bytes 663560 | tf_op jit(solution)/shard_map/ppermute | solution.py:15
  66.2 31.5 %copy-start.13 = (f32[48,1,25]{0,2,1:T(8,128)}, f32[48,1,25]{0,2,1:T(8,128)S(1)}, u32[]{:S(2)}) copy-start(f32[48,1,25]{0,2,1:T(8,128)S(1)} %get-tuple-element.70) | copy-start | bytes 14404
  66.2 31.5 %copy-start.15 = (f32[48,1,25]{0,2,1:T(8,128)}, f32[48,1,25]{0,2,1:T(8,128)S(1)}, u32[]{:S(2)}) copy-start(f32[48,1,25]{0,2,1:T(8,128)S(1)} %get-tuple-element.71) | copy-start | bytes 14404
  83.8 13.1 %copy-start.7 = (bf16[1,48,2304]{2,0,1:T(2,128)(2,1)}, bf16[1,48,2304]{2,0,1:T(2,128)(2,1)S(1)}, u32[]{:S(2)}) copy-start(bf16[1,48,2304]{2,0,1:T(2,128)(2,1)S(1)} %collective-permute-done.5) | copy-start | bytes 663556
  92.9 4.1 %copy-start.8 = (bf16[1,48,2304]{2,0,1:T(2,128)(2,1)}, bf16[1,48,2304]{2,0,1:T(2,128)(2,1)S(1)}, u32[]{:S(2)}) copy-start(bf16[1,48,2304]{2,0,1:T(2,128)(2,1)S(1)} %collective-permute-done.2) | copy-start | bytes 663556
  114.7 3.7 %copy-start.14 = (f32[48,1,25]{0,2,1:T(8,128)S(1)}, f32[48,1,25]{0,2,1:T(8,128)}, u32[]{:S(2)}) copy-start(f32[48,1,25]{0,2,1:T(8,128)} %copy-done.13) | copy-start | bytes 14404
  114.7 3.7 %copy-start.16 = (f32[48,1,25]{0,2,1:T(8,128)S(1)}, f32[48,1,25]{0,2,1:T(8,128)}, u32[]{:S(2)}) copy-start(f32[48,1,25]{0,2,1:T(8,128)} %copy-done.15) | copy-start | bytes 14404
  125.6 2.2 %copy-start.12 = (f32[2,48,2,48]{1,3,2,0:T(8,128)S(1)}, f32[2,48,2,48]{1,3,2,0:T(8,128)}, u32[]{:S(2)}) copy-start(f32[2,48,2,48]{1,3,2,0:T(8,128)} %copy-done.11) | copy-start | bytes 110596
  127.7 1.2 copy-start.10
  135.1 1.2 copy-start.1
  135.1 1.2 copy-start.3
  135.1 1.2 copy-start.5
  135.1 1.3 copy-start.6
  136.4 3.6 %copy-start.17 = (u32[32]{0:T(128)S(1)}, u32[32]{0:T(128)}, u32[]{:S(2)}) copy-start(u32[32]{0:T(128)} %constant.103) | copy-start | bytes 388
Sparse Core Ops, SparseCore 0:
  140.1 31.1 all-reduce.2
where the time goes:
time: 183 us; the launch traced here: 180 us
  waiting for transfers between devices  83.5 us (46%)
  matrix products  30.8 us (17%)
  starting transfers between devices  28.1 us (15%)
  between operations  14.6 us (8%)
  local copies, waits for them, and re-layouts  12 us (7%)
  other arithmetic  11 us (6%)
    ppermute x6, waiting for transfers between devices, from_behind(): return lax.ppermute(block, axis, route)  53.4 us
    dot_general x12, matrix products, contract(): return jnp.einsum(form, data, table, precision=lax.Precision.HIGHEST)  30.8 us
    unnamed x2, waiting for transfers between devices  30 us
    ppermute x6, starting transfers between devices, from_behind(): return lax.ppermute(block, axis, route)  28.1 us
    mul x1, other arithmetic, step(): left_band.reshape(1, grid_edge, grid_edge, grid_edge) * right_cubes  4.06 us
    unnamed x39, local copies, waits for them, and re-layouts  3.67 us
  transfers between devices with their start and end apart: 7, of which 6 were waited for; matrix products, arithmetic and copies ran while one was open for 2% of the time, Pallas kernels for 0%

commit v1 on v0

v1 whole, which is shorter than its diff:
```python
import functools
import math

import jax
import jax.numpy as jnp
import numpy as np
from jax import lax
from jax.experimental import pallas as pl
from jax.experimental.pallas import tpu as pltpu
from jax.sharding import PartitionSpec as P

cell_edge = 59.0
screen_rate = 0.106
lanes = 128
half = lanes // 2


def signed_points(grid_edge):
    points = np.arange(grid_edge)
    return np.where(points > grid_edge // 2, points - grid_edge, points)


def real_basis(grid_edge):
    points = np.arange(grid_edge)
    angles = 2.0 * np.pi / grid_edge * (points[:, None] * points[None, :] % grid_edge)
    rows = np.where(points[:, None] <= grid_edge // 2, np.cos(angles), np.sin(angles))
    single = (points == 0) | (2 * points == grid_edge)
    return rows * np.sqrt(np.where(single, 1.0, 2.0) / grid_edge)[:, None]


def in_two(values):
    high = values.astype(jnp.bfloat16)
    low = (values - high.astype(np.float64)).astype(jnp.bfloat16)
    return high, low


def left_table(matrix):
    high, low = in_two(matrix)
    return np.concatenate([high, high, low], axis=1)


def right_table(matrix):
    edge = matrix.shape[0]
    both = np.zeros((lanes, lanes))
    both[:edge, :edge] = matrix
    both[half : half + edge, half : half + edge] = matrix
    high, low = in_two(both)
    return np.block([[high, low], [high, np.zeros_like(low)]])


def screened_kernel(grid_edge):
    signed = signed_points(grid_edge)
    row = np.zeros(lanes, np.int32)
    row[:grid_edge] = signed**2
    row[half : half + grid_edge] = signed**2
    squares = jnp.asarray(signed**2, jnp.int32)
    squared = squares[:, None, None] + squares[None, :, None] + jnp.asarray(row)[None, None, :]
    wave_sq = squared.astype(jnp.float32) * jnp.float32((2.0 * math.pi / cell_edge) ** 2)
    safe_sq = jnp.where(squared == 0, jnp.float32(1.0), wave_sq)
    screened = 4.0 * math.pi * -jnp.expm1(-safe_sq / (4.0 * screen_rate**2)) / safe_sq
    return jnp.where(squared == 0, jnp.float32(math.pi / screen_rate**2), screened)


def split(values):
    high = values.astype(jnp.bfloat16)
    low = (values - high.astype(jnp.float32)).astype(jnp.bfloat16)
    return high, low


def dot(left, right):
    return jnp.dot(left, right, preferred_element_type=jnp.float32)


def rows_transform(table, slabs):
    done = []
    for first in range(0, len(slabs), 2):
        columns = []
        for slab in slabs[first : first + 2]:
            high, low = split(slab)
            columns.append(jnp.concatenate([high, low, high], axis=0))
        product = dot(table, jnp.concatenate(columns, axis=1))
        for k in range(len(columns)):
            done.append(product[:, k * lanes : (k + 1) * lanes])
    return done


def lanes_transform(slabs, table):
    edge = slabs[0].shape[0]
    high, low = split(jnp.concatenate(slabs, axis=0))
    product = dot(jnp.concatenate([high, low], axis=1), table)
    product = product[:, :lanes] + product[:, lanes:]
    return [product[k * edge : (k + 1) * edge] for k in range(len(slabs))]


def pair_kernel(
    grid_edge, slots, order_ref, home_ref, ahead_ref, behind_ref, kernel_ref,
    left_fwd_ref, left_back_ref, right_fwd_ref, right_back_ref, near_ref, far_ref, work, result,
):
    group = lanes // math.gcd(lanes, grid_edge)
    width = group * grid_edge
    tiles = width // lanes
    planes = grid_edge // slots
    lane = lax.broadcasted_iota(jnp.int32, (grid_edge, lanes), 1)

    def tiles_of(ref, start):
        return [
            ref[:, pl.ds(pl.multiple_of(start + t * lanes, lanes), lanes)].astype(jnp.float32)
            for t in range(tiles)
        ]

    def turn(values, amount):
        amount %= lanes
        return pltpu.roll(values, amount, 1) if amount else values

    @pl.loop(0, grid_edge // group)
    def _(block):
        start = block * width
        home = tiles_of(home_ref, start)
        first = [a * b for a, b in zip(home, tiles_of(ahead_ref, start))]
        second = [turn(a * b, half) for a, b in zip(home, tiles_of(behind_ref, start))]
        slabs = []
        for k in range(group):
            tile, offset = divmod(k * grid_edge, lanes)
            in_first = ((lane + (lanes - offset)) % lanes) < half
            this_a, this_b = first[tile], second[tile]
            if offset + grid_edge > lanes:
                this_a = jnp.where(lane >= offset, this_a, first[tile + 1])
                from_this = ((lane + half) % lanes) >= offset
                this_b = jnp.where(from_this, this_b, second[tile + 1])
            slabs.append(turn(jnp.where(in_first, this_a, this_b), -offset))
        slabs = lanes_transform(slabs, right_fwd_ref[...])
        slabs = rows_transform(left_fwd_ref[...], slabs)
        for k, slab in enumerate(slabs):
            at = pl.multiple_of((block * group + k) * grid_edge, grid_edge)
            work[pl.ds(at, grid_edge), :] = slab

    together = 8 if grid_edge % 8 == 0 else 1

    @pl.loop(0, grid_edge // together)
    def _(block):
        rows = [pl.ds(block * together + k, grid_edge, stride=grid_edge) for k in range(together)]
        slabs = rows_transform(left_fwd_ref[...], [work[r, :] for r in rows])
        slabs = [slab * kernel_ref[block * together + k] for k, slab in enumerate(slabs)]
        slabs = rows_transform(left_back_ref[...], slabs)
        for r, slab in zip(rows, slabs):
            work[r, :] = slab

    @pl.loop(0, grid_edge // group)
    def _(block):
        start = block * width
        slabs = []
        for k in range(group):
            at = pl.multiple_of((block * group + k) * grid_edge, grid_edge)
            slabs.append(work[pl.ds(at, grid_edge), :])
        slabs = rows_transform(left_back_ref[...], slabs)
        slabs = lanes_transform(slabs, right_back_ref[...])
        slabs = [turn(slab, k * grid_edge) for k, slab in enumerate(slabs)]
        ahead = tiles_of(ahead_ref, start)
        behind = tiles_of(behind_ref, start)
        for t in range(tiles):
            sources = range(t * lanes // grid_edge, ((t + 1) * lanes - 1) // grid_edge + 1)
            dense_a = dense_b = slabs[sources[0]]
            shifted = (lane + half) % lanes
            for k in sources[1:]:
                edge_lane = k * grid_edge - t * lanes
                dense_a = jnp.where(lane >= edge_lane, slabs[k], dense_a)
                dense_b = jnp.where(shifted >= edge_lane, slabs[k], dense_b)
            total = -0.25 * (dense_a * ahead[t] + turn(dense_b, half) * behind[t])
            columns = pl.ds(pl.multiple_of(start + t * lanes, lanes), lanes)
            for p in range(slots):
                result[order_ref[p], :, columns] = total[p * planes : (p + 1) * planes]

    for k in range(slots // 2):
        near_ref[k] = result[2 * k]
        far_ref[k] = result[2 * k + 1]


def pair_terms(order, home, ahead, behind, kernel):
    grid_edge, plane_size = home.shape
    slots = order.shape[0]
    basis = real_basis(grid_edge)
    tables = (left_table(basis), left_table(basis.T), right_table(basis.T), right_table(basis))
    part = jax.ShapeDtypeStruct((slots // 2, grid_edge // slots, plane_size), jnp.float32)
    vmem = pl.BlockSpec(memory_space=pltpu.VMEM)
    return pl.pallas_call(
        functools.partial(pair_kernel, grid_edge, slots),
        out_shape=(part, part),
        in_specs=[pl.BlockSpec(memory_space=pltpu.SMEM)] + [vmem] * 8,
        out_specs=(vmem, vmem),
        scratch_shapes=[
            pltpu.VMEM((grid_edge * grid_edge, lanes), jnp.float32),
            pltpu.VMEM((slots, grid_edge // slots, plane_size), jnp.float32),
        ],
        compiler_params=pltpu.CompilerParams(vmem_limit_bytes=32 * 1024 * 1024),
        cost_estimate=pl.CostEstimate(flops=2 * 10**9, bytes_accessed=3 * 10**6, transcendentals=0),
    )(order, home, ahead, behind, kernel, *(jnp.asarray(t) for t in tables))


def offsets_of(cycle_size, groups):
    bits = groups.bit_length() - 1
    turned = [int(format(g, "b").zfill(bits)[::-1], 2) if bits else 0 for g in range(groups)]
    ahead = [d if d else cycle_size // 2 for d in turned]
    behind = [-d for d in turned]
    return ahead, behind


def fetch(block, offsets, cycle_size, groups):
    route = []
    for blk in range(cycle_size):
        for g in range(groups):
            if offsets[g] % cycle_size:
                route.append(((blk + offsets[g]) % cycle_size * groups + g, blk * groups + g))
    return lax.ppermute(block, ("blk", "off"), route)


def scattered_sum(near, far, groups):
    bit = 1
    while True:
        arrived = lax.ppermute(far, "off", [(g, g ^ bit) for g in range(groups)])
        near = near + arrived
        bit *= 2
        if bit == groups:
            return near[0]
        near, far = near[0::2], near[1::2]


def on_device(orbitals):
    band_count, grid_edge, plane_size = orbitals.shape
    cycle_size, groups = lax.axis_size("blk"), lax.axis_size("off")
    if cycle_size != 2 * groups or groups & (groups - 1) or groups < 2:
        raise ValueError("unsupported mesh")
    me = lax.axis_index("off")
    ahead_offsets, behind_offsets = offsets_of(cycle_size, groups)
    behind = fetch(orbitals, behind_offsets, cycle_size, groups)
    ahead = fetch(orbitals, ahead_offsets, cycle_size, groups)
    behind = jnp.where(me == 0, orbitals, behind)
    kernel = screened_kernel(grid_edge)
    order = jnp.arange(groups, dtype=jnp.int32) ^ me
    rows = []
    for i in range(band_count):
        near = far = 0.0
        for j in range(band_count):
            terms = pair_terms(order, orbitals[i], ahead[j], behind[j], kernel)
            near, far = near + terms[0], far + terms[1]
        rows.append(scattered_sum(near, far, groups))
    return jnp.stack(rows)


def solution(mesh):
    return jax.shard_map(
        on_device,
        mesh=mesh,
        in_specs=(P("blk", None, None),),
        out_specs=P("blk", "off", None),
        check_vma=False,
    )
```

time: 183 us -> 35.3 us (0.19); the launches traced: 180 us -> 35.1 us
  waiting for transfers between devices: 83.5 us -> 13.5 us
  matrix products: 30.8 us -> 0 us
  starting transfers between devices: 28.1 us -> 9.51 us
  between operations: 14.6 us -> 0.1 us
  local copies, waits for them, and re-layouts: 12 us -> 0.79 us
  Pallas kernels: 0 us -> 8.89 us
  other arithmetic: 11 us -> 2.32 us
    ppermute x6 -> x4, waiting for transfers between devices: 53.4 us -> 13.5 us  [the longest x2 7.57 us: fetch(): return lax.ppermute(block, ('blk', 'off'), route)]
    dot_general x12 -> x0, matrix products: 30.8 us -> none  [contract(): return jnp.einsum(form, data, table, precision=lax.Precision.HIGHEST)]
    unnamed x2 -> x0, waiting for transfers between devices: 30 us -> none
    ppermute x6 -> x4, starting transfers between devices: 28.1 us -> 9.51 us  [the longest x2 4.8 us: fetch(): return lax.ppermute(block, ('blk', 'off'), route)]
    pallas_call x0 -> x1, Pallas kernels: none -> 8.89 us  [pair_terms(): pl.pallas_call(functools.partial(pair_kernel, grid_edge, slots), out_shap...]
    mul x3 -> x0, other arithmetic: 7.64 us -> none  [the longest x1 4.06 us: step(): left_band.reshape(1, grid_edge, grid_edge, grid_edge) * right_cubes]
    unnamed x39 -> x10, local copies, waits for them, and re-layouts: 3.67 us -> 0.02 us
    reshape x2 -> x0, local copies, waits for them, and re-layouts: 3.1 us -> none  [step(): potential(densities, tables, kernel)]
  transfers between devices with their start and end apart: 7 -> 4, of which waited for: 6 -> 3; matrix products, arithmetic and copies ran while one was open for 2% -> 6% of each run, Pallas kernels for 0% -> 0%
where the time goes in v1:
time: 35.3 us; the launch traced here: 35.1 us
  waiting for transfers between devices  13.5 us (38%)
  starting transfers between devices  9.51 us (27%)
  Pallas kernels  8.89 us (25%)
  other arithmetic  2.32 us (7%)
  local copies, waits for them, and re-layouts  0.79 us (2%)
    pallas_call x1, Pallas kernels, pair_terms(): pl.pallas_call(functools.partial(pair_kernel, grid_edge, slots), out_shap...  8.89 us
    ppermute x2, waiting for transfers between devices, fetch(): return lax.ppermute(block, ('blk', 'off'), route)  7.57 us
    ppermute x2, waiting for transfers between devices, scattered_sum(): arrived = lax.ppermute(far, 'off', [(g, g ^ bit) for g in range(groups)])  5.96 us
    ppermute x2, starting transfers between devices, fetch(): return lax.ppermute(block, ('blk', 'off'), route)  4.8 us
    ppermute x2, starting transfers between devices, scattered_sum(): arrived = lax.ppermute(far, 'off', [(g, g ^ bit) for g in range(groups)])  4.71 us
    select_n x1, other arithmetic, screened_kernel(): jnp.where(squared == 0, jnp.float32(math.pi / screen_rate ** 2), screened)  1.41 us
    add x1, other arithmetic, screened_kernel(): squares[:, None, None] + squares[None, :, None]  0.81 us
    add x1, local copies, waits for them, and re-layouts, scattered_sum(): near = near + arrived  0.76 us
  transfers between devices with their start and end apart: 4, of which 3 were waited for; matrix products, arithmetic and copies ran while one was open for 6% of the time, Pallas kernels for 0%

profile of v1, /device:TPU:0, one launch (start us, length us, event | category | flops | bytes accessed | tf_op | source)
XLA Modules:
  0.0 35.1 jit_solution(85409621306894794)
XLA Ops:
  0.0 0.0 copy-start.1
  0.0 0.0 copy-start.2
  0.0 0.0 copy-start.3
  0.0 0.0 copy-start.4
  0.0 0.0 copy-start
  0.0 4.1 %collective-permute-start = (bf16[1,48,2304]{2,1,0:T(8,128)(2,1)}, bf16[1,48,2304]{2,1,0:T(8,128)(2,1)S(1)}, u32[]{:S(2)}, u32[]{:S(2)}) collective-permute-start(bf16[1,48,2304]{2,1,0:T(8,128)(2,1)} %param.7), channel_id=1, source_target_pairs={{16,0},{9,1},{6,2},{15,3},{20,4},{13,5},{10,6},{19,7},{24,8},{17,9... | collective-permute-start | bytes 663560 | tf_op jit(solution)/shard_map/ppermute | solution.py:213
  4.1 0.7 %collective-permute-start.1 = (bf16[1,48,2304]{2,1,0:T(8,128)(2,1)}, bf16[1,48,2304]{2,1,0:T(8,128)(2,1)S(1)}, u32[]{:S(2)}, u32[]{:S(2)}) collective-permute-start(bf16[1,48,2304]{2,1,0:T(8,128)(2,1)} %param.7), channel_id=1, source_target_pairs={{25,1},{30,2},{23,3},{29,5},{2,6},{27,7},{1,9},{6,10},{31,11},{5,1... | collective-permute-start | bytes 663560 | tf_op jit(solution)/shard_map/ppermute | solution.py:213
  4.8 0.8 %broadcast_add_fusion = s32[48,48]{1,0:T(8,128)S(1)} fusion(s32[48]{0:T(128)} %constant.30.clone), kind=kLoop, calls=%fused_computation.13 | loop fusion | flops 2304 | bytes 9408 | tf_op jit(solution)/shard_map/add | solution.py:57
  5.6 1.4 %fusion.kernel_ref = f32[48,48,128]{2,1,0:T(8,128)S(1)} fusion(s32[128]{0:T(128)} %constant.31.clone, s32[48,48]{1,0:T(8,128)S(1)} %broadcast_add_fusion), kind=kLoop, calls=%fused_computation.2 | loop fusion | flops 3244032 | bytes 1189376 | tf_op jit(solution)/shard_map/jit(_where)/select_n | solution.py:61
  7.1 0.0 collective-permute-done.1
  7.1 0.0 copy-done
  7.1 7.6 %collective-permute-done = bf16[1,48,2304]{2,1,0:T(8,128)(2,1)S(1)} collective-permute-done((bf16[1,48,2304]{2,1,0:T(8,128)(2,1)}, bf16[1,48,2304]{2,1,0:T(8,128)(2,1)S(1)}, u32[]{:S(2)}, u32[]{:S(2)}) %collective-permute-start) | collective-permute-done | bytes 221216 | tf_op jit(solution)/shard_map/ppermute | solution.py:213
  14.7 0.0 copy-done.1
  14.7 0.0 copy-done.2
  14.7 0.0 copy-done.3
  14.7 0.0 copy-done.4
  14.7 8.9 %shard_map.73 = (f32[2,12,2304]{2,1,0:T(8,128)S(1)}, f32[2,12,2304]{2,1,0:T(8,128)S(1)}) custom-call(s32[4]{0:T(128)S(1)} %iota_xor_fusion.order_ref, bf16[48,2304]{1,0:T(8,128)(2,1)S(1)} %bitcast.4, bf16[48,2304]{1,0:T(8,128)(2,1)S(1)} %bitcast.5, bf16[48,2304]{1,0:T(8,128)(2,1)S(1)} %select_bitcast_fusion.behind_ref, f32[48,48,128]{2,1,0:T(8,128)S(1)} %fusion.kernel_ref, ...), custom_call_target="tpu_custom_call" | custom-call | flops 2000000000 | bytes 3000000 | tf_op jit(solution)/shard_map/pallas_call | solution.py:185
  23.6 0.1 collective-permute-start.2
  23.7 1.6 %collective-permute-done.2 = f32[2,12,2304]{2,1,0:T(8,128)S(1)} collective-permute-done((f32[2,12,2304]{2,1,0:T(8,128)S(1)}, f32[2,12,2304]{2,1,0:T(8,128)S(1)}, u32[]{:S(2)}, u32[]{:S(2)}) %collective-permute-start.2) | collective-permute-done | bytes 221216 | tf_op jit(solution)/shard_map/ppermute | solution.py:219
  25.3 4.6 %collective-permute-start.3 = (f32[1,12,2304]{2,1,0:T(8,128)S(1)}, f32[1,12,2304]{2,1,0:T(8,128)S(1)}, u32[]{:S(2)}, u32[]{:S(2)}) collective-permute-start(f32[1,12,2304]{2,1,0:T(8,128)S(1)} %slice.11), channel_id=1, source_target_pairs={{0,2},{1,3},{2,0},{3,1},{4,6},{5,7},{6,4},{7,5},{8,10},{9,11},{10,... | collective-permute-start | bytes 331784 | tf_op jit(solution)/shard_map/ppermute | solution.py:219
  30.0 4.4 %collective-permute-done.3 = f32[1,12,2304]{2,1,0:T(8,128)S(1)} collective-permute-done((f32[1,12,2304]{2,1,0:T(8,128)S(1)}, f32[1,12,2304]{2,1,0:T(8,128)S(1)}, u32[]{:S(2)}, u32[]{:S(2)}) %collective-permute-start.3) | collective-permute-done | bytes 110624 | tf_op jit(solution)/shard_map/ppermute | solution.py:219
  34.4 0.8 %copy.8 = f32[1,12,2304]{2,0,1:T(1,128)} copy(f32[1,12,2304]{2,1,0:T(8,128)S(1)} %slice_add_fusion) | data formatting | bytes 221184 | tf_op jit(solution)/shard_map/add | solution.py:220
  (5 shorter events, 0.1 us)
Async XLA Ops:
  0.0 14.7 %copy-start.1 = (bf16[256,256]{1,0:T(8,128)(2,1)S(1)}, bf16[256,256]{1,0:T(8,128)(2,1)}, u32[]{:S(2)}) copy-start(bf16[256,256]{1,0:T(8,128)(2,1)} %constant.35.clone.right_back_ref) | copy-start | bytes 393220
  0.0 14.7 %copy-start.2 = (bf16[256,256]{1,0:T(8,128)(2,1)S(1)}, bf16[256,256]{1,0:T(8,128)(2,1)}, u32[]{:S(2)}) copy-start(bf16[256,256]{1,0:T(8,128)(2,1)} %constant.34.clone.right_fwd_ref) | copy-start | bytes 393220
  0.0 14.7 %copy-start.3 = (bf16[48,144]{1,0:T(8,128)(2,1)S(1)}, bf16[48,144]{1,0:T(8,128)(2,1)}, u32[]{:S(2)}) copy-start(bf16[48,144]{1,0:T(8,128)(2,1)} %constant.33.clone.left_back_ref) | copy-start | bytes 41476
  0.0 14.7 %copy-start.4 = (bf16[48,144]{1,0:T(8,128)(2,1)S(1)}, bf16[48,144]{1,0:T(8,128)(2,1)}, u32[]{:S(2)}) copy-start(bf16[48,144]{1,0:T(8,128)(2,1)} %constant.32.clone.left_fwd_ref) | copy-start | bytes 41476
  0.0 7.1 %copy-start = (bf16[1,48,2304]{2,1,0:T(8,128)(2,1)S(1)}, bf16[1,48,2304]{2,1,0:T(8,128)(2,1)}, u32[]{:S(2)}) copy-start(bf16[1,48,2304]{2,1,0:T(8,128)(2,1)} %param.7) | copy-start | bytes 663556
  0.0 14.7 %collective-permute-start = (bf16[1,48,2304]{2,1,0:T(8,128)(2,1)}, bf16[1,48,2304]{2,1,0:T(8,128)(2,1)S(1)}, u32[]{:S(2)}, u32[]{:S(2)}) collective-permute-start(bf16[1,48,2304]{2,1,0:T(8,128)(2,1)} %param.7), channel_id=1, source_target_pairs={{16,0},{9,1},{6,2},{15,3},{20,4},{13,5},{10,6},{19,7},{24,8},{17,9... | collective-permute-start | bytes 663560 | tf_op jit(solution)/shard_map/ppermute | solution.py:213
  4.1 2.9 %collective-permute-start.1 = (bf16[1,48,2304]{2,1,0:T(8,128)(2,1)}, bf16[1,48,2304]{2,1,0:T(8,128)(2,1)S(1)}, u32[]{:S(2)}, u32[]{:S(2)}) collective-permute-start(bf16[1,48,2304]{2,1,0:T(8,128)(2,1)} %param.7), channel_id=1, source_target_pairs={{25,1},{30,2},{23,3},{29,5},{2,6},{27,7},{1,9},{6,10},{31,11},{5,1... | collective-permute-start | bytes 663560 | tf_op jit(solution)/shard_map/ppermute | solution.py:213
  23.6 1.6 %collective-permute-start.2 = (f32[2,12,2304]{2,1,0:T(8,128)S(1)}, f32[2,12,2304]{2,1,0:T(8,128)S(1)}, u32[]{:S(2)}, u32[]{:S(2)}) collective-permute-start(f32[2,12,2304]{2,1,0:T(8,128)S(1)} %get-tuple-element.8), channel_id=1, source_target_pairs={{0,1},{1,0},{2,3},{3,2},{4,5},{5,4},{6,7},{7,6},{8,9},{9,8},{10,11... | collective-permute-start | bytes 663560 | tf_op jit(solution)/shard_map/ppermute | solution.py:219
  25.3 9.0 %collective-permute-start.3 = (f32[1,12,2304]{2,1,0:T(8,128)S(1)}, f32[1,12,2304]{2,1,0:T(8,128)S(1)}, u32[]{:S(2)}, u32[]{:S(2)}) collective-permute-start(f32[1,12,2304]{2,1,0:T(8,128)S(1)} %slice.11), channel_id=1, source_target_pairs={{0,2},{1,3},{2,0},{3,1},{4,6},{5,7},{6,4},{7,5},{8,10},{9,11},{10,... | collective-permute-start | bytes 331784 | tf_op jit(solution)/shard_map/ppermute | solution.py:219

commit v2 on v1

--- a/solution.py
+++ b/solution.py
@@ -94,17 +94,20 @@
 
 def pair_kernel(
     grid_edge, slots, order_ref, home_ref, ahead_ref, behind_ref, kernel_ref,
-    left_fwd_ref, left_back_ref, right_fwd_ref, right_back_ref, near_ref, far_ref, work, result,
+    left_fwd_ref, left_back_ref, right_fwd_ref, right_back_ref, near_ref, far_ref, work, back, result,
 ):
     group = lanes // math.gcd(lanes, grid_edge)
-    width = group * grid_edge
-    tiles = width // lanes
+    tiles = group * grid_edge // lanes
+    pitch = work.shape[0] // grid_edge
     planes = grid_edge // slots
+    row_tiles = grid_edge * grid_edge // lanes
     lane = lax.broadcasted_iota(jnp.int32, (grid_edge, lanes), 1)
-
-    def tiles_of(ref, start):
+    shifted = (lane + half) % lanes
+
+    def tiles_of(ref, block):
+        first = block * tiles
         return [
-            ref[:, pl.ds(pl.multiple_of(start + t * lanes, lanes), lanes)].astype(jnp.float32)
+            ref[:, (first + t) * lanes : (first + t + 1) * lanes].astype(jnp.float32)
             for t in range(tiles)
         ]
 
@@ -112,12 +115,10 @@
         amount %= lanes
         return pltpu.roll(values, amount, 1) if amount else values
 
-    @pl.loop(0, grid_edge // group)
-    def _(block):
-        start = block * width
-        home = tiles_of(home_ref, start)
-        first = [a * b for a, b in zip(home, tiles_of(ahead_ref, start))]
-        second = [turn(a * b, half) for a, b in zip(home, tiles_of(behind_ref, start))]
+    for block in range(grid_edge // group):
+        home = tiles_of(home_ref, block)
+        first = [a * b for a, b in zip(home, tiles_of(ahead_ref, block))]
+        second = [turn(a * b, half) for a, b in zip(home, tiles_of(behind_ref, block))]
         slabs = []
         for k in range(group):
             tile, offset = divmod(k * grid_edge, lanes)
@@ -125,50 +126,39 @@
             this_a, this_b = first[tile], second[tile]
             if offset + grid_edge > lanes:
                 this_a = jnp.where(lane >= offset, this_a, first[tile + 1])
-                from_this = ((lane + half) % lanes) >= offset
-                this_b = jnp.where(from_this, this_b, second[tile + 1])
+                this_b = jnp.where(shifted >= offset, this_b, second[tile + 1])
             slabs.append(turn(jnp.where(in_first, this_a, this_b), -offset))
         slabs = lanes_transform(slabs, right_fwd_ref[...])
         slabs = rows_transform(left_fwd_ref[...], slabs)
         for k, slab in enumerate(slabs):
-            at = pl.multiple_of((block * group + k) * grid_edge, grid_edge)
-            work[pl.ds(at, grid_edge), :] = slab
-
-    together = 8 if grid_edge % 8 == 0 else 1
-
-    @pl.loop(0, grid_edge // together)
-    def _(block):
-        rows = [pl.ds(block * together + k, grid_edge, stride=grid_edge) for k in range(together)]
+            work[pl.ds((block * group + k) * pitch, grid_edge), :] = slab
+
+    for block in range(grid_edge // group):
+        rows = [pl.ds(block * group + k, grid_edge, stride=pitch) for k in range(group)]
         slabs = rows_transform(left_fwd_ref[...], [work[r, :] for r in rows])
-        slabs = [slab * kernel_ref[block * together + k] for k, slab in enumerate(slabs)]
+        slabs = [slab * kernel_ref[block * group + k] for k, slab in enumerate(slabs)]
         slabs = rows_transform(left_back_ref[...], slabs)
         for r, slab in zip(rows, slabs):
-            work[r, :] = slab
-
-    @pl.loop(0, grid_edge // group)
-    def _(block):
-        start = block * width
-        slabs = []
-        for k in range(group):
-            at = pl.multiple_of((block * group + k) * grid_edge, grid_edge)
-            slabs.append(work[pl.ds(at, grid_edge), :])
+            back[r, :] = slab
+
+    for block in range(grid_edge // group):
+        slabs = [back[pl.ds((block * group + k) * pitch, grid_edge), :] for k in range(group)]
         slabs = rows_transform(left_back_ref[...], slabs)
         slabs = lanes_transform(slabs, right_back_ref[...])
         slabs = [turn(slab, k * grid_edge) for k, slab in enumerate(slabs)]
-        ahead = tiles_of(ahead_ref, start)
-        behind = tiles_of(behind_ref, start)
+        ahead = tiles_of(ahead_ref, block)
+        behind = tiles_of(behind_ref, block)
         for t in range(tiles):
             sources = range(t * lanes // grid_edge, ((t + 1) * lanes - 1) // grid_edge + 1)
             dense_a = dense_b = slabs[sources[0]]
-            shifted = (lane + half) % lanes
             for k in sources[1:]:
                 edge_lane = k * grid_edge - t * lanes
                 dense_a = jnp.where(lane >= edge_lane, slabs[k], dense_a)
                 dense_b = jnp.where(shifted >= edge_lane, slabs[k], dense_b)
             total = -0.25 * (dense_a * ahead[t] + turn(dense_b, half) * behind[t])
-            columns = pl.ds(pl.multiple_of(start + t * lanes, lanes), lanes)
+            rows = pl.ds(block * tiles + t, planes, stride=row_tiles)
             for p in range(slots):
-                result[order_ref[p], :, columns] = total[p * planes : (p + 1) * planes]
+                result[order_ref[p], rows, :] = total[p * planes : (p + 1) * planes]
 
     for k in range(slots // 2):
         near_ref[k] = result[2 * k]
@@ -180,7 +170,9 @@
     slots = order.shape[0]
     basis = real_basis(grid_edge)
     tables = (left_table(basis), left_table(basis.T), right_table(basis.T), right_table(basis))
-    part = jax.ShapeDtypeStruct((slots // 2, grid_edge // slots, plane_size), jnp.float32)
+    slot_rows = grid_edge // slots * plane_size // lanes
+    pitch = -(-grid_edge // 8) * 8 + 4
+    part = jax.ShapeDtypeStruct((slots // 2, slot_rows, lanes), jnp.float32)
     vmem = pl.BlockSpec(memory_space=pltpu.VMEM)
     return pl.pallas_call(
         functools.partial(pair_kernel, grid_edge, slots),
@@ -188,8 +180,9 @@
         in_specs=[pl.BlockSpec(memory_space=pltpu.SMEM)] + [vmem] * 8,
         out_specs=(vmem, vmem),
         scratch_shapes=[
-            pltpu.VMEM((grid_edge * grid_edge, lanes), jnp.float32),
-            pltpu.VMEM((slots, grid_edge // slots, plane_size), jnp.float32),
+            pltpu.VMEM((grid_edge * pitch, lanes), jnp.float32),
+            pltpu.VMEM((grid_edge * pitch, lanes), jnp.float32),
+            pltpu.VMEM((slots, slot_rows, lanes), jnp.float32),
         ],
         compiler_params=pltpu.CompilerParams(vmem_limit_bytes=32 * 1024 * 1024),
         cost_estimate=pl.CostEstimate(flops=2 * 10**9, bytes_accessed=3 * 10**6, transcendentals=0),
@@ -227,7 +220,7 @@
 def on_device(orbitals):
     band_count, grid_edge, plane_size = orbitals.shape
     cycle_size, groups = lax.axis_size("blk"), lax.axis_size("off")
-    if cycle_size != 2 * groups or groups & (groups - 1) or groups < 2:
+    if cycle_size != 2 * groups or groups & (groups - 1) or groups < 2 or grid_edge > half:
         raise ValueError("unsupported mesh")
     me = lax.axis_index("off")
     ahead_offsets, behind_offsets = offsets_of(cycle_size, groups)
@@ -243,7 +236,7 @@
             terms = pair_terms(order, orbitals[i], ahead[j], behind[j], kernel)
             near, far = near + terms[0], far + terms[1]
         rows.append(scattered_sum(near, far, groups))
-    return jnp.stack(rows)
+    return jnp.stack(rows).reshape(band_count, grid_edge // groups, plane_size)
 
 
 def solution(mesh):

time: 35.3 us -> 29.8 us (0.84)
  Pallas kernels: 8.89 us -> 4.45 us
  waiting for transfers between devices: 13.5 us -> 12.6 us
  local copies, waits for them, and re-layouts: 0.79 us -> 0.03 us
  other arithmetic: 2.32 us -> 2.95 us
    pallas_call x1, Pallas kernels: 8.89 us -> 4.45 us  [pair_terms(): pl.pallas_call(functools.partial(pair_kernel, grid_edge, slots), out_shap...]
    ppermute x2, waiting for transfers between devices: 5.96 us -> 5.06 us  [scattered_sum(): arrived = lax.ppermute(far, 'off', [(g, g ^ bit) for g in range(groups)])]
    add x1 -> x0, local copies, waits for them, and re-layouts: 0.76 us -> none  [scattered_sum(): near = near + arrived]
    add x2, other arithmetic: 0.06 us -> 0.69 us  [scattered_sum(): near = near + arrived]
  transfers between devices with their start and end apart: 4 -> 4, of which waited for: 3 -> 3; matrix products, arithmetic and copies ran while one was open for 6% -> 8% of each run, Pallas kernels for 0% -> 0%
where the time goes in v2:
time: 29.8 us; the launch traced here: 29.7 us
  waiting for transfers between devices  12.6 us (42%)
  starting transfers between devices  9.5 us (32%)
  Pallas kernels  4.45 us (15%)
  other arithmetic  2.95 us (10%)
    ppermute x2, waiting for transfers between devices, fetch(): return lax.ppermute(block, ('blk', 'off'), route)  7.57 us
    ppermute x2, waiting for transfers between devices, scattered_sum(): arrived = lax.ppermute(far, 'off', [(g, g ^ bit) for g in range(groups)])  5.06 us
    ppermute x2, starting transfers between devices, fetch(): return lax.ppermute(block, ('blk', 'off'), route)  4.8 us
    ppermute x2, starting transfers between devices, scattered_sum(): arrived = lax.ppermute(far, 'off', [(g, g ^ bit) for g in range(groups)])  4.71 us
    pallas_call x1, Pallas kernels, pair_terms(): pl.pallas_call(functools.partial(pair_kernel, grid_edge, slots), out_shap...  4.45 us
    select_n x1, other arithmetic, screened_kernel(): jnp.where(squared == 0, jnp.float32(math.pi / screen_rate ** 2), screened)  1.41 us
    add x1, other arithmetic, screened_kernel(): squares[:, None, None] + squares[None, :, None]  0.81 us
    add x2, other arithmetic, scattered_sum(): near = near + arrived  0.69 us
  transfers between devices with their start and end apart: 4, of which 3 were waited for; matrix products, arithmetic and copies ran while one was open for 8% of the time, Pallas kernels for 0%

profile of v2, /device:TPU:0, one launch (start us, length us, event | category | flops | bytes accessed | tf_op | source)
XLA Modules:
  0.0 29.7 jit_solution(10544769103206410085)
XLA Ops:
  0.0 0.0 copy-start.1
  0.0 0.0 copy-start.2
  0.0 0.0 copy-start.3
  0.0 0.0 copy-start.4
  0.0 0.0 copy-start
  0.0 4.1 %collective-permute-start = (bf16[1,48,2304]{2,1,0:T(8,128)(2,1)}, bf16[1,48,2304]{2,1,0:T(8,128)(2,1)S(1)}, u32[]{:S(2)}, u32[]{:S(2)}) collective-permute-start(bf16[1,48,2304]{2,1,0:T(8,128)(2,1)} %param.7), channel_id=1, source_target_pairs={{16,0},{9,1},{6,2},{15,3},{20,4},{13,5},{10,6},{19,7},{24,8},{17,9... | collective-permute-start | bytes 663560 | tf_op jit(solution)/shard_map/ppermute | solution.py:206
  4.1 0.7 %collective-permute-start.1 = (bf16[1,48,2304]{2,1,0:T(8,128)(2,1)}, bf16[1,48,2304]{2,1,0:T(8,128)(2,1)S(1)}, u32[]{:S(2)}, u32[]{:S(2)}) collective-permute-start(bf16[1,48,2304]{2,1,0:T(8,128)(2,1)} %param.7), channel_id=1, source_target_pairs={{25,1},{30,2},{23,3},{29,5},{2,6},{27,7},{1,9},{6,10},{31,11},{5,1... | collective-permute-start | bytes 663560 | tf_op jit(solution)/shard_map/ppermute | solution.py:206
  4.8 0.8 %broadcast_add_fusion = s32[48,48]{1,0:T(8,128)S(1)} fusion(s32[48]{0:T(128)} %constant.30.clone), kind=kLoop, calls=%fused_computation.13 | loop fusion | flops 2304 | bytes 9408 | tf_op jit(solution)/shard_map/add | solution.py:57
  5.6 1.4 %fusion.kernel_ref = f32[48,48,128]{2,1,0:T(8,128)S(1)} fusion(s32[128]{0:T(128)} %constant.31.clone, s32[48,48]{1,0:T(8,128)S(1)} %broadcast_add_fusion), kind=kLoop, calls=%fused_computation.2 | loop fusion | flops 3244032 | bytes 1189376 | tf_op jit(solution)/shard_map/jit(_where)/select_n | solution.py:61
  7.1 0.0 collective-permute-done.1
  7.1 0.0 copy-done
  7.1 7.6 %collective-permute-done = bf16[1,48,2304]{2,1,0:T(8,128)(2,1)S(1)} collective-permute-done((bf16[1,48,2304]{2,1,0:T(8,128)(2,1)}, bf16[1,48,2304]{2,1,0:T(8,128)(2,1)S(1)}, u32[]{:S(2)}, u32[]{:S(2)}) %collective-permute-start) | collective-permute-done | bytes 221216 | tf_op jit(solution)/shard_map/ppermute | solution.py:206
  14.7 0.0 copy-done.1
  14.7 0.0 copy-done.2
  14.7 0.0 copy-done.3
  14.7 0.0 copy-done.4
  14.7 4.4 %shard_map.73 = (f32[2,216,128]{2,1,0:T(8,128)S(1)}, f32[2,216,128]{2,1,0:T(8,128)S(1)}) custom-call(s32[4]{0:T(128)S(1)} %iota_xor_fusion.order_ref, bf16[48,2304]{1,0:T(8,128)(2,1)S(1)} %bitcast.5, bf16[48,2304]{1,0:T(8,128)(2,1)S(1)} %bitcast.6, bf16[48,2304]{1,0:T(8,128)(2,1)S(1)} %select_bitcast_fusion.behind_ref, f32[48,48,128]{2,1,0:T(8,128)S(1)} %fusion.kernel_ref, ...), custom_call_target="tpu_custom_call" | custom-call | flops 2000000000 | bytes 3000000 | tf_op jit(solution)/shard_map/pallas_call | solution.py:177
  19.2 0.1 collective-permute-start.2
  19.2 1.5 %collective-permute-done.2 = f32[2,216,128]{2,1,0:T(8,128)S(1)} collective-permute-done((f32[2,216,128]{2,1,0:T(8,128)S(1)}, f32[2,216,128]{2,1,0:T(8,128)S(1)}, u32[]{:S(2)}, u32[]{:S(2)}) %collective-permute-start.2) | collective-permute-done | bytes 221216 | tf_op jit(solution)/shard_map/ppermute | solution.py:212
  20.8 4.6 %collective-permute-start.3 = (f32[1,216,128]{2,1,0:T(8,128)S(1)}, f32[1,216,128]{2,1,0:T(8,128)S(1)}, u32[]{:S(2)}, u32[]{:S(2)}) collective-permute-start(f32[1,216,128]{2,1,0:T(8,128)S(1)} %slice.11), channel_id=1, source_target_pairs={{0,2},{1,3},{2,0},{3,1},{4,6},{5,7},{6,4},{7,5},{8,10},{9,11},{10,... | collective-permute-start | bytes 331784 | tf_op jit(solution)/shard_map/ppermute | solution.py:212
  25.4 3.6 %collective-permute-done.3 = f32[1,216,128]{2,1,0:T(8,128)S(1)} collective-permute-done((f32[1,216,128]{2,1,0:T(8,128)S(1)}, f32[1,216,128]{2,1,0:T(8,128)S(1)}, u32[]{:S(2)}, u32[]{:S(2)}) %collective-permute-start.3) | collective-permute-done | bytes 110624 | tf_op jit(solution)/shard_map/ppermute | solution.py:212
  29.0 0.7 %slice_add_fusion = f32[1,216,128]{2,1,0:T(8,128)} fusion(f32[1,216,128]{2,1,0:T(8,128)S(1)} %collective-permute-done.3, f32[2,216,128]{2,1,0:T(8,128)S(1)} %add.43), kind=kLoop, calls=%fused_computation.12 | loop fusion | flops 27648 | bytes 331776 | tf_op jit(solution)/shard_map/add | solution.py:213
  (4 shorter events, 0.1 us)
Async XLA Ops:
  0.0 14.7 %copy-start.1 = (bf16[256,256]{1,0:T(8,128)(2,1)S(1)}, bf16[256,256]{1,0:T(8,128)(2,1)}, u32[]{:S(2)}) copy-start(bf16[256,256]{1,0:T(8,128)(2,1)} %constant.35.clone.right_back_ref) | copy-start | bytes 393220
  0.0 14.7 %copy-start.2 = (bf16[256,256]{1,0:T(8,128)(2,1)S(1)}, bf16[256,256]{1,0:T(8,128)(2,1)}, u32[]{:S(2)}) copy-start(bf16[256,256]{1,0:T(8,128)(2,1)} %constant.34.clone.right_fwd_ref) | copy-start | bytes 393220
  0.0 14.7 %copy-start.3 = (bf16[48,144]{1,0:T(8,128)(2,1)S(1)}, bf16[48,144]{1,0:T(8,128)(2,1)}, u32[]{:S(2)}) copy-start(bf16[48,144]{1,0:T(8,128)(2,1)} %constant.33.clone.left_back_ref) | copy-start | bytes 41476
  0.0 14.7 %copy-start.4 = (bf16[48,144]{1,0:T(8,128)(2,1)S(1)}, bf16[48,144]{1,0:T(8,128)(2,1)}, u32[]{:S(2)}) copy-start(bf16[48,144]{1,0:T(8,128)(2,1)} %constant.32.clone.left_fwd_ref) | copy-start | bytes 41476
  0.0 7.1 %copy-start = (bf16[1,48,2304]{2,1,0:T(8,128)(2,1)S(1)}, bf16[1,48,2304]{2,1,0:T(8,128)(2,1)}, u32[]{:S(2)}) copy-start(bf16[1,48,2304]{2,1,0:T(8,128)(2,1)} %param.7) | copy-start | bytes 663556
  0.0 14.7 %collective-permute-start = (bf16[1,48,2304]{2,1,0:T(8,128)(2,1)}, bf16[1,48,2304]{2,1,0:T(8,128)(2,1)S(1)}, u32[]{:S(2)}, u32[]{:S(2)}) collective-permute-start(bf16[1,48,2304]{2,1,0:T(8,128)(2,1)} %param.7), channel_id=1, source_target_pairs={{16,0},{9,1},{6,2},{15,3},{20,4},{13,5},{10,6},{19,7},{24,8},{17,9... | collective-permute-start | bytes 663560 | tf_op jit(solution)/shard_map/ppermute | solution.py:206
  4.1 2.9 %collective-permute-start.1 = (bf16[1,48,2304]{2,1,0:T(8,128)(2,1)}, bf16[1,48,2304]{2,1,0:T(8,128)(2,1)S(1)}, u32[]{:S(2)}, u32[]{:S(2)}) collective-permute-start(bf16[1,48,2304]{2,1,0:T(8,128)(2,1)} %param.7), channel_id=1, source_target_pairs={{25,1},{30,2},{23,3},{29,5},{2,6},{27,7},{1,9},{6,10},{31,11},{5,1... | collective-permute-start | bytes 663560 | tf_op jit(solution)/shard_map/ppermute | solution.py:206
  19.2 1.5 %collective-permute-start.2 = (f32[2,216,128]{2,1,0:T(8,128)S(1)}, f32[2,216,128]{2,1,0:T(8,128)S(1)}, u32[]{:S(2)}, u32[]{:S(2)}) collective-permute-start(f32[2,216,128]{2,1,0:T(8,128)S(1)} %get-tuple-element.8), channel_id=1, source_target_pairs={{0,1},{1,0},{2,3},{3,2},{4,5},{5,4},{6,7},{7,6},{8,9},{9,8},{10,11... | collective-permute-start | bytes 663560 | tf_op jit(solution)/shard_map/ppermute | solution.py:212
  20.8 8.2 %collective-permute-start.3 = (f32[1,216,128]{2,1,0:T(8,128)S(1)}, f32[1,216,128]{2,1,0:T(8,128)S(1)}, u32[]{:S(2)}, u32[]{:S(2)}) collective-permute-start(f32[1,216,128]{2,1,0:T(8,128)S(1)} %slice.11), channel_id=1, source_target_pairs={{0,2},{1,3},{2,0},{3,1},{4,6},{5,7},{6,4},{7,5},{8,10},{9,11},{10,... | collective-permute-start | bytes 331784 | tf_op jit(solution)/shard_map/ppermute | solution.py:212

commit v3 on v2

v3 whole, which is shorter than its diff:
```python
import functools
import math

import jax
import jax.numpy as jnp
import numpy as np
from jax import lax
from jax.experimental import pallas as pl
from jax.experimental.pallas import tpu as pltpu
from jax.sharding import PartitionSpec as P

cell_edge = 59.0
screen_rate = 0.106
lanes = 128
together_blocks = 2
half = lanes // 2


def signed_points(grid_edge):
    points = np.arange(grid_edge)
    return np.where(points > grid_edge // 2, points - grid_edge, points)


def real_basis(grid_edge):
    points = np.arange(grid_edge)
    angles = 2.0 * np.pi / grid_edge * (points[:, None] * points[None, :] % grid_edge)
    rows = np.where(points[:, None] <= grid_edge // 2, np.cos(angles), np.sin(angles))
    single = (points == 0) | (2 * points == grid_edge)
    return rows * np.sqrt(np.where(single, 1.0, 2.0) / grid_edge)[:, None]


def in_two(values):
    high = values.astype(jnp.bfloat16)
    low = (values - high.astype(np.float64)).astype(jnp.bfloat16)
    return high, low


def left_table(matrix):
    high, low = in_two(matrix)
    return np.concatenate([high, high, low], axis=1)


def right_table(matrix, start_in, start_out):
    edge = matrix.shape[0]
    both = np.zeros((lanes, lanes))
    both[:edge, :edge] = matrix
    both[start_in : start_in + edge, start_out : start_out + edge] = matrix
    high, low = in_two(both)
    return np.block([[high, low], [high, np.zeros_like(low)]])


def screened_kernel(grid_edge):
    signed = signed_points(grid_edge)
    row = np.zeros(lanes, np.int32)
    row[:grid_edge] = signed**2
    row[half : half + grid_edge] = signed**2
    pair = np.where(np.arange(lanes) < half, signed[0::2, None] ** 2, signed[1::2, None] ** 2) + row
    squared = jnp.asarray(pair, jnp.int32)[:, None, :] + jnp.asarray(signed**2, jnp.int32)[None, :, None]
    wave_sq = squared.astype(jnp.float32) * jnp.float32((2.0 * math.pi / cell_edge) ** 2)
    safe_sq = jnp.where(squared == 0, jnp.float32(1.0), wave_sq)
    screened = 4.0 * math.pi * -jnp.expm1(-safe_sq / (4.0 * screen_rate**2)) / safe_sq
    return jnp.where(squared == 0, jnp.float32(math.pi / screen_rate**2), screened)


def split(values):
    high = values.astype(jnp.bfloat16)
    low = (values - high.astype(jnp.float32)).astype(jnp.bfloat16)
    return high, low


def dot(left, right):
    return jnp.dot(left, right, preferred_element_type=jnp.float32)


def rows_products(table, slabs):
    done = []
    for first in range(0, len(slabs), 2):
        columns = []
        for slab in slabs[first : first + 2]:
            high, low = split(slab)
            columns.append(jnp.concatenate([high, low, high], axis=0))
        product = dot(table, jnp.concatenate(columns, axis=1))
        done += [product[:, k * lanes : (k + 1) * lanes] for k in range(len(columns))]
    return done


def lanes_product(slabs, table):
    high, low = split(jnp.concatenate(slabs, axis=0))
    return dot(jnp.concatenate([high, low], axis=1), table)


def lanes_result(product, count):
    edge = product.shape[0] // count
    product = product[:, :lanes] + product[:, lanes:]
    return [product[k * edge : (k + 1) * edge] for k in range(count)]


def in_steps(count, *steps):
    held = [{} for _ in steps]
    for time in range(count + len(steps) - 1):
        for n, step in enumerate(steps):
            item = time - n
            if 0 <= item < count:
                given = (held[n - 1].pop(item),) if n else ()
                held[n][item] = step(item, *given)


def pair_kernel(grid_edge, slots, has_prior, last, *refs):
    refs = list(refs)
    order_ref, home_ref, other_ref, kernel_ref = refs[:4]
    left_first_ref, left_fwd_ref, left_back_ref, left_last_ref, right_fwd_ref, right_back_ref = refs[4:10]
    prior_ref = refs[10] if has_prior else None
    outs = refs[10 + has_prior : -2 - last]
    work, back = refs[-2 - last], refs[-1 - last]
    result = refs[-1] if last else outs[0]

    line = 2 * grid_edge
    group = lanes // math.gcd(lanes, line)
    tiles = group * line // lanes
    pitch = work.shape[0] // (grid_edge // 2)
    planes = grid_edge // slots
    row_tiles = grid_edge * grid_edge // lanes
    lane = lax.broadcasted_iota(jnp.int32, (grid_edge, lanes), 1)
    together = together_blocks if grid_edge % (2 * together_blocks) == 0 else 1
    in_first = lax.broadcasted_iota(jnp.int32, (grid_edge // 2, lanes), 1) < half

    def tiles_of(ref, block):
        first = block * tiles
        return [
            ref[:, (first + t) * lanes : (first + t + 1) * lanes].astype(jnp.float32)
            for t in range(tiles)
        ]

    def turn(values, amount):
        amount %= lanes
        return pltpu.roll(values, amount, 1) if amount else values

    def first_lanes(block):
        dense = [a * b for a, b in zip(tiles_of(home_ref, block), tiles_of(other_ref, block))]
        slabs = []
        for k in range(group):
            tile, offset = divmod(k * line, lanes)
            slab = dense[tile]
            if offset + line > lanes:
                slab = jnp.where(lane >= offset, slab, dense[tile + 1])
            slabs.append(turn(slab, -offset))
        return lanes_product(slabs, right_fwd_ref[...])

    def first_rows(block, product):
        return rows_products(left_first_ref[...], lanes_result(product, group))

    def first_store(block, slabs):
        for k, slab in enumerate(slabs):
            work[pl.ds((block * group + k) * pitch, grid_edge), :] = slab

    in_steps(grid_edge // 2 // group, first_lanes, first_rows, first_store)

    def rows_of(block):
        start = 2 * block * together
        return [
            [pl.ds(start + 2 * k + d, grid_edge // 2, stride=pitch) for d in range(2)]
            for k in range(together)
        ]

    def middle_forward(block):
        slabs = []
        for pair in rows_of(block):
            even, odd = (work[r, :] for r in pair)
            top = jnp.where(in_first, even, turn(odd, half))
            bottom = jnp.where(in_first, turn(even, half), odd)
            slabs.append(jnp.concatenate([top, bottom], axis=0))
        return rows_products(left_fwd_ref[...], slabs)

    def middle_back(block, slabs):
        slabs = [slab * kernel_ref[block * together + k] for k, slab in enumerate(slabs)]
        return rows_products(left_back_ref[...], slabs)

    def middle_store(block, slabs):
        for (row_even, row_odd), slab in zip(rows_of(block), slabs):
            top, bottom = slab[: grid_edge // 2], slab[grid_edge // 2 :]
            back[row_even, :] = jnp.where(in_first, top, turn(bottom, half))
            back[row_odd, :] = jnp.where(in_first, turn(top, half), bottom)

    in_steps(grid_edge // 2 // together, middle_forward, middle_back, middle_store)

    def last_rows(block):
        slabs = [back[pl.ds((block * group + k) * pitch, grid_edge), :] for k in range(group)]
        return rows_products(left_last_ref[...], slabs)

    def last_lanes(block, slabs):
        return lanes_product(slabs, right_back_ref[...])

    def last_store(block, product):
        slabs = [turn(slab, k * line) for k, slab in enumerate(lanes_result(product, group))]
        other = tiles_of(other_ref, block)
        for t in range(tiles):
            sources = range(t * lanes // line, ((t + 1) * lanes - 1) // line + 1)
            dense = slabs[sources[0]]
            for k in sources[1:]:
                dense = jnp.where(lane >= k * line - t * lanes, slabs[k], dense)
            total = -0.25 * (dense * other[t])
            rows = pl.ds(block * tiles + t, planes, stride=row_tiles)
            for p in range(slots):
                result[order_ref[p], rows, :] = total[p * planes : (p + 1) * planes]

    in_steps(grid_edge // 2 // group, last_rows, last_lanes, last_store)

    if last:
        for k in range(slots):
            terms = result[k]
            if has_prior:
                terms += prior_ref[k]
            outs[k % 2][k // 2] = terms
    elif has_prior:
        result[...] += prior_ref[...]


def pair_terms(order, home, other, kernel, prior, last):
    grid_edge, plane_size = home.shape
    slots = order.shape[0]
    basis = real_basis(grid_edge)
    mixed = np.concatenate([np.arange(0, grid_edge, 2), np.arange(1, grid_edge, 2)])
    tables = (
        left_table(basis),
        left_table(basis[:, mixed]),
        left_table(basis.T[mixed]),
        left_table(basis.T),
        right_table(basis.T, grid_edge, half),
        right_table(basis, half, grid_edge),
    )
    slot_rows = grid_edge // slots * plane_size // lanes
    pitch = -(-grid_edge // 8) * 8 + 4
    whole = jax.ShapeDtypeStruct((slots, slot_rows, lanes), jnp.float32)
    part = jax.ShapeDtypeStruct((slots // 2, slot_rows, lanes), jnp.float32)
    vmem = pl.BlockSpec(memory_space=pltpu.VMEM)
    operands = [order, home, other, kernel, *(jnp.asarray(t) for t in tables)]
    operands += [] if prior is None else [prior]
    scratch = [pltpu.VMEM((grid_edge // 2 * pitch, lanes), jnp.float32)] * 2
    scratch += [pltpu.VMEM(whole.shape, jnp.float32)] if last else []
    return pl.pallas_call(
        functools.partial(pair_kernel, grid_edge, slots, prior is not None, last),
        out_shape=(part, part) if last else whole,
        in_specs=[pl.BlockSpec(memory_space=pltpu.SMEM)] + [vmem] * (len(operands) - 1),
        out_specs=(vmem, vmem) if last else vmem,
        scratch_shapes=scratch,
        compiler_params=pltpu.CompilerParams(vmem_limit_bytes=32 * 1024 * 1024),
        cost_estimate=pl.CostEstimate(flops=10**9, bytes_accessed=2 * 10**6, transcendentals=0),
    )(*operands)


def fetch(block, masks, cycle_size, groups):
    route = []
    for blk in range(cycle_size):
        for g in range(groups):
            if masks[g]:
                route.append(((blk ^ masks[g]) * groups + g, blk * groups + g))
    return lax.ppermute(block, ("blk", "off"), route)


def scattered_sum(near, far, groups):
    bit = 1
    while True:
        arrived = lax.ppermute(far, "off", [(g, g ^ bit) for g in range(groups)])
        near = near + arrived
        bit *= 2
        if bit == groups:
            return near[0]
        near, far = near[0::2], near[1::2]


def on_device(orbitals):
    band_count, grid_edge, plane_size = orbitals.shape
    cycle_size, groups = lax.axis_size("blk"), lax.axis_size("off")
    if cycle_size != 2 * groups or groups & (groups - 1) or groups < 2 or grid_edge > half:
        raise ValueError("unsupported mesh")
    me = lax.axis_index("off")
    early = fetch(orbitals, list(range(groups)), cycle_size, groups)
    late = fetch(orbitals, list(range(groups, cycle_size)), cycle_size, groups)
    early = jnp.where(me == 0, orbitals, early)
    kernel = screened_kernel(grid_edge)
    order = jnp.arange(groups, dtype=jnp.int32) ^ me
    rows = []
    for home in orbitals:
        others = [*early, *late]
        terms = None
        for other in others[:-1]:
            terms = pair_terms(order, home, other, kernel, terms, False)
        near, far = pair_terms(order, home, others[-1], kernel, terms, True)
        rows.append(scattered_sum(near, far, groups))
    return jnp.stack(rows).reshape(band_count, grid_edge // groups, plane_size)


def solution(mesh):
    return jax.shard_map(
        on_device,
        mesh=mesh,
        in_specs=(P("blk", None, None),),
        out_specs=P("blk", "off", None),
        check_vma=False,
    )
```

time: 29.8 us -> 29.1 us (0.977)
  waiting for transfers between devices: 12.6 us -> 10.6 us
  other arithmetic: 2.95 us -> 1.14 us
  local copies, waits for them, and re-layouts: 0.03 us -> 1.57 us
  starting transfers between devices: 9.5 us -> 10.4 us
  Pallas kernels: 4.45 us -> 5.17 us
    ppermute x2, waiting for transfers between devices: 7.57 us -> 5.73 us  [fetch(): return lax.ppermute(block, ('blk', 'off'), route)]
    unnamed x10 -> x18, local copies, waits for them, and re-layouts: 0.02 us -> 1.56 us
    select_n x1, other arithmetic: 1.41 us -> 0.41 us  [screened_kernel(): jnp.where(squared == 0, jnp.float32(math.pi / screen_rate ** 2), screened)]
    ppermute x2, starting transfers between devices: 4.71 us -> 5.62 us  [scattered_sum(): arrived = lax.ppermute(far, 'off', [(g, g ^ bit) for g in range(groups)])]
    add x1 -> x0, other arithmetic: 0.81 us -> none  [screened_kernel(): squares[:, None, None] + squares[None, :, None]]
    pallas_call x1 -> x2, Pallas kernels: 4.45 us -> 5.17 us  [pair_terms(): pl.pallas_call(functools.partial(pair_kernel, grid_edge, slots, prior is...]
  transfers between devices with their start and end apart: 4 -> 4, of which waited for: 3 -> 3; matrix products, arithmetic and copies ran while one was open for 8% -> 2% of each run, Pallas kernels for 0% -> 9%
where the time goes in v3:
time: 29.1 us; the launch traced here: 28.9 us
  waiting for transfers between devices  10.6 us (36%)
  starting transfers between devices  10.4 us (36%)
  Pallas kernels  5.17 us (18%)
  local copies, waits for them, and re-layouts  1.57 us (5%)
  other arithmetic  1.14 us (4%)
    ppermute x2, waiting for transfers between devices, fetch(): return lax.ppermute(block, ('blk', 'off'), route)  5.73 us
    ppermute x2, starting transfers between devices, scattered_sum(): arrived = lax.ppermute(far, 'off', [(g, g ^ bit) for g in range(groups)])  5.62 us
    pallas_call x2, Pallas kernels, pair_terms(): pl.pallas_call(functools.partial(pair_kernel, grid_edge, slots, prior is...  5.17 us
    ppermute x2, waiting for transfers between devices, scattered_sum(): arrived = lax.ppermute(far, 'off', [(g, g ^ bit) for g in range(groups)])  4.82 us
    ppermute x2, starting transfers between devices, fetch(): return lax.ppermute(block, ('blk', 'off'), route)  4.73 us
    unnamed x18, local copies, waits for them, and re-layouts  1.56 us
    add x2, other arithmetic, scattered_sum(): near = near + arrived  0.69 us
  transfers between devices with their start and end apart: 4, of which 3 were waited for; matrix products, arithmetic and copies ran while one was open for 2% of the time, Pallas kernels for 9%

profile of v3, /device:TPU:0, one launch (start us, length us, event | category | flops | bytes accessed | tf_op | source)
XLA Modules:
  0.0 28.9 jit_solution(7215670946524118631)
XLA Ops:
  0.0 0.0 copy-start.7
  0.0 4.1 %collective-permute-start = (bf16[1,48,2304]{2,1,0:T(8,128)(2,1)}, bf16[1,48,2304]{2,1,0:T(8,128)(2,1)S(1)}, u32[]{:S(2)}, u32[]{:S(2)}) collective-permute-start(bf16[1,48,2304]{2,1,0:T(8,128)(2,1)} %param.15), channel_id=1, source_target_pairs={{16,0},{21,1},{26,2},{31,3},{20,4},{17,5},{30,6},{27,7},{24,8},{29... | collective-permute-start | bytes 663560 | tf_op jit(solution)/shard_map/ppermute | solution.py:257
  4.1 0.7 %collective-permute-start.1 = (bf16[1,48,2304]{2,1,0:T(8,128)(2,1)}, bf16[1,48,2304]{2,1,0:T(8,128)(2,1)S(1)}, u32[]{:S(2)}, u32[]{:S(2)}) collective-permute-start(bf16[1,48,2304]{2,1,0:T(8,128)(2,1)} %param.15), channel_id=1, source_target_pairs={{5,1},{10,2},{15,3},{1,5},{14,6},{11,7},{13,9},{2,10},{7,11},{9,13... | collective-permute-start | bytes 663560 | tf_op jit(solution)/shard_map/ppermute | solution.py:257
  4.8 0.0 copy-start.8
  4.8 0.0 copy-done.7
  4.8 0.6 %copy-done.8 = s32[48]{0:T(128)S(1)} copy-done((s32[48]{0:T(128)S(1)}, s32[48]{0:T(128)}, u32[]{:S(2)}) %copy-start.8) | copy-done | bytes 216
  5.4 0.0 copy-start
  5.4 0.4 %fusion.refs_3_ = f32[24,48,128]{2,1,0:T(8,128)S(1)} fusion(s32[48]{0:T(128)S(1)} %copy-done.8, s32[24,128]{1,0:T(8,128)S(1)} %copy-done.7), kind=kLoop, calls=%fused_computation.2 | loop fusion | flops 1622016 | bytes 602304 | tf_op jit(solution)/shard_map/jit(_where)/select_n | solution.py:62
  5.8 0.0 copy-start.1
  5.8 0.0 copy-start.2
  5.9 0.0 copy-start.3
  5.9 0.0 copy-start.4
  5.9 0.0 copy-start.5
  5.9 0.0 copy-start.6
  5.9 0.0 collective-permute-done.1
  5.9 0.4 %copy-done = bf16[1,48,2304]{2,1,0:T(8,128)(2,1)S(1)} copy-done((bf16[1,48,2304]{2,1,0:T(8,128)(2,1)S(1)}, bf16[1,48,2304]{2,1,0:T(8,128)(2,1)}, u32[]{:S(2)}) %copy-start) | copy-done | bytes 221208
  6.4 0.4 %copy-done.1 = bf16[256,256]{1,0:T(8,128)(2,1)S(1)} copy-done((bf16[256,256]{1,0:T(8,128)(2,1)S(1)}, bf16[256,256]{1,0:T(8,128)(2,1)}, u32[]{:S(2)}) %copy-start.1) | copy-done | bytes 131096
  6.8 0.1 copy-done.2
  6.8 0.0 copy-done.3
  6.8 0.0 copy-done.4
  6.8 0.0 copy-done.5
  6.8 0.0 copy-done.6
  6.8 2.6 %shard_map.145.refs_10_ = f32[4,216,128]{2,1,0:T(8,128)S(1)} custom-call(s32[4]{0:T(128)S(1)} %iota_xor_fusion.refs_0_, bf16[48,2304]{1,0:T(8,128)(2,1)S(1)} %bitcast.5, bf16[48,2304]{1,0:T(8,128)(2,1)S(1)} %select_bitcast_fusion.refs_2_, f32[24,48,128]{2,1,0:T(8,128)S(1)} %fusion.refs_3_, bf16[48,144]{1,0:T(8,128)(2,1)S(1)} %copy-done.6, ...), custom_call_target="tpu_custom_call" | custom-call | flops 1000000000 | bytes 2000000 | tf_op jit(solution)/shard_map/pallas_call | solution.py:240
  9.4 5.7 %collective-permute-done = bf16[1,48,2304]{2,1,0:T(8,128)(2,1)S(1)} collective-permute-done((bf16[1,48,2304]{2,1,0:T(8,128)(2,1)}, bf16[1,48,2304]{2,1,0:T(8,128)(2,1)S(1)}, u32[]{:S(2)}, u32[]{:S(2)}) %collective-permute-start) | collective-permute-done | bytes 221216 | tf_op jit(solution)/shard_map/ppermute | solution.py:257
  15.1 2.6 %shard_map.146 = (f32[2,216,128]{2,1,0:T(8,128)S(1)}, f32[2,216,128]{2,1,0:T(8,128)S(1)}) custom-call(s32[4]{0:T(128)S(1)} %iota_xor_fusion.refs_0_, bf16[48,2304]{1,0:T(8,128)(2,1)S(1)} %bitcast.6, bf16[48,2304]{1,0:T(8,128)(2,1)S(1)} %bitcast.7, f32[24,48,128]{2,1,0:T(8,128)S(1)} %fusion.refs_3_, bf16[48,144]{1,0:T(8,128)(2,1)S(1)} %copy-done.6, ...), custom_call_target="tpu_custom_call" | custom-call | flops 1000000000 | bytes 2000000 | tf_op jit(solution)/shard_map/pallas_call | solution.py:240
  17.7 0.1 collective-permute-start.2
  17.8 1.5 %collective-permute-done.2 = f32[2,216,128]{2,1,0:T(8,128)S(1)} collective-permute-done((f32[2,216,128]{2,1,0:T(8,128)S(1)}, f32[2,216,128]{2,1,0:T(8,128)S(1)}, u32[]{:S(2)}, u32[]{:S(2)}) %collective-permute-start.2) | collective-permute-done | bytes 221216 | tf_op jit(solution)/shard_map/ppermute | solution.py:263
  19.3 5.6 %collective-permute-start.3 = (f32[1,216,128]{2,1,0:T(8,128)S(1)}, f32[1,216,128]{2,1,0:T(8,128)S(1)}, u32[]{:S(2)}, u32[]{:S(2)}) collective-permute-start(f32[1,216,128]{2,1,0:T(8,128)S(1)} %slice.11), channel_id=1, source_target_pairs={{0,2},{1,3},{2,0},{3,1},{4,6},{5,7},{6,4},{7,5},{8,10},{9,11},{10,... | collective-permute-start | bytes 331784 | tf_op jit(solution)/shard_map/ppermute | solution.py:263
  24.9 3.4 %collective-permute-done.3 = f32[1,216,128]{2,1,0:T(8,128)S(1)} collective-permute-done((f32[1,216,128]{2,1,0:T(8,128)S(1)}, f32[1,216,128]{2,1,0:T(8,128)S(1)}, u32[]{:S(2)}, u32[]{:S(2)}) %collective-permute-start.3) | collective-permute-done | bytes 110624 | tf_op jit(solution)/shard_map/ppermute | solution.py:263
  28.3 0.7 %slice_add_fusion = f32[1,216,128]{2,1,0:T(8,128)} fusion(f32[1,216,128]{2,1,0:T(8,128)S(1)} %collective-permute-done.3, f32[2,216,128]{2,1,0:T(8,128)S(1)} %add.22), kind=kLoop, calls=%fused_computation.12 | loop fusion | flops 27648 | bytes 331776 | tf_op jit(solution)/shard_map/add | solution.py:264
  (4 shorter events, 0.1 us)
Async XLA Ops:
  0.0 4.8 %copy-start.7 = (s32[24,128]{1,0:T(8,128)S(1)}, s32[24,128]{1,0:T(8,128)}, u32[]{:S(2)}) copy-start(s32[24,128]{1,0:T(8,128)} %constant.34.clone) | copy-start | bytes 36868
  0.0 15.1 %collective-permute-start = (bf16[1,48,2304]{2,1,0:T(8,128)(2,1)}, bf16[1,48,2304]{2,1,0:T(8,128)(2,1)S(1)}, u32[]{:S(2)}, u32[]{:S(2)}) collective-permute-start(bf16[1,48,2304]{2,1,0:T(8,128)(2,1)} %param.15), channel_id=1, source_target_pairs={{16,0},{21,1},{26,2},{31,3},{20,4},{17,5},{30,6},{27,7},{24,8},{29... | collective-permute-start | bytes 663560 | tf_op jit(solution)/shard_map/ppermute | solution.py:257
  4.1 1.8 %collective-permute-start.1 = (bf16[1,48,2304]{2,1,0:T(8,128)(2,1)}, bf16[1,48,2304]{2,1,0:T(8,128)(2,1)S(1)}, u32[]{:S(2)}, u32[]{:S(2)}) collective-permute-start(bf16[1,48,2304]{2,1,0:T(8,128)(2,1)} %param.15), channel_id=1, source_target_pairs={{5,1},{10,2},{15,3},{1,5},{14,6},{11,7},{13,9},{2,10},{7,11},{9,13... | collective-permute-start | bytes 663560 | tf_op jit(solution)/shard_map/ppermute | solution.py:257
  4.8 0.7 %copy-start.8 = (s32[48]{0:T(128)S(1)}, s32[48]{0:T(128)}, u32[]{:S(2)}) copy-start(s32[48]{0:T(128)} %constant.35.clone) | copy-start | bytes 580
  5.4 0.9 %copy-start = (bf16[1,48,2304]{2,1,0:T(8,128)(2,1)S(1)}, bf16[1,48,2304]{2,1,0:T(8,128)(2,1)}, u32[]{:S(2)}) copy-start(bf16[1,48,2304]{2,1,0:T(8,128)(2,1)} %param.15) | copy-start | bytes 663556
  5.8 0.9 %copy-start.1 = (bf16[256,256]{1,0:T(8,128)(2,1)S(1)}, bf16[256,256]{1,0:T(8,128)(2,1)}, u32[]{:S(2)}) copy-start(bf16[256,256]{1,0:T(8,128)(2,1)} %constant.41.clone.refs_9_) | copy-start | bytes 393220
  5.8 1.0 %copy-start.2 = (bf16[256,256]{1,0:T(8,128)(2,1)S(1)}, bf16[256,256]{1,0:T(8,128)(2,1)}, u32[]{:S(2)}) copy-start(bf16[256,256]{1,0:T(8,128)(2,1)} %constant.40.clone.refs_8_) | copy-start | bytes 393220
  5.9 1.0 %copy-start.3 = (bf16[48,144]{1,0:T(8,128)(2,1)S(1)}, bf16[48,144]{1,0:T(8,128)(2,1)}, u32[]{:S(2)}) copy-start(bf16[48,144]{1,0:T(8,128)(2,1)} %constant.39.clone.refs_7_) | copy-start | bytes 41476
  5.9 1.0 %copy-start.4 = (bf16[48,144]{1,0:T(8,128)(2,1)S(1)}, bf16[48,144]{1,0:T(8,128)(2,1)}, u32[]{:S(2)}) copy-start(bf16[48,144]{1,0:T(8,128)(2,1)} %constant.38.clone.refs_6_) | copy-start | bytes 41476
  5.9 1.0 %copy-start.5 = (bf16[48,144]{1,0:T(8,128)(2,1)S(1)}, bf16[48,144]{1,0:T(8,128)(2,1)}, u32[]{:S(2)}) copy-start(bf16[48,144]{1,0:T(8,128)(2,1)} %constant.37.clone.refs_5_) | copy-start | bytes 41476
  5.9 0.9 %copy-start.6 = (bf16[48,144]{1,0:T(8,128)(2,1)S(1)}, bf16[48,144]{1,0:T(8,128)(2,1)}, u32[]{:S(2)}) copy-start(bf16[48,144]{1,0:T(8,128)(2,1)} %constant.36.clone.refs_4_) | copy-start | bytes 41476
  17.7 1.5 %collective-permute-start.2 = (f32[2,216,128]{2,1,0:T(8,128)S(1)}, f32[2,216,128]{2,1,0:T(8,128)S(1)}, u32[]{:S(2)}, u32[]{:S(2)}) collective-permute-start(f32[2,216,128]{2,1,0:T(8,128)S(1)} %get-tuple-element.8), channel_id=1, source_target_pairs={{0,1},{1,0},{2,3},{3,2},{4,5},{5,4},{6,7},{7,6},{8,9},{9,8},{10,11... | collective-permute-start | bytes 663560 | tf_op jit(solution)/shard_map/ppermute | solution.py:263
  19.3 8.9 %collective-permute-start.3 = (f32[1,216,128]{2,1,0:T(8,128)S(1)}, f32[1,216,128]{2,1,0:T(8,128)S(1)}, u32[]{:S(2)}, u32[]{:S(2)}) collective-permute-start(f32[1,216,128]{2,1,0:T(8,128)S(1)} %slice.11), channel_id=1, source_target_pairs={{0,2},{1,3},{2,0},{3,1},{4,6},{5,7},{6,4},{7,5},{8,10},{9,11},{10,... | collective-permute-start | bytes 331784 | tf_op jit(solution)/shard_map/ppermute | solution.py:263

commit v4 on v2

--- a/solution.py
+++ b/solution.py
@@ -8,6 +8,7 @@
 from jax.experimental import pallas as pl
 from jax.experimental.pallas import tpu as pltpu
 from jax.sharding import PartitionSpec as P
+
 
 cell_edge = 59.0
 screen_rate = 0.106
@@ -71,7 +72,7 @@
     return jnp.dot(left, right, preferred_element_type=jnp.float32)
 
 
-def rows_transform(table, slabs):
+def rows_products(table, slabs):
     done = []
     for first in range(0, len(slabs), 2):
         columns = []
@@ -79,17 +80,29 @@
             high, low = split(slab)
             columns.append(jnp.concatenate([high, low, high], axis=0))
         product = dot(table, jnp.concatenate(columns, axis=1))
-        for k in range(len(columns)):
-            done.append(product[:, k * lanes : (k + 1) * lanes])
+        done += [product[:, k * lanes : (k + 1) * lanes] for k in range(len(columns))]
     return done
 
 
-def lanes_transform(slabs, table):
-    edge = slabs[0].shape[0]
+def lanes_product(slabs, table):
     high, low = split(jnp.concatenate(slabs, axis=0))
-    product = dot(jnp.concatenate([high, low], axis=1), table)
+    return dot(jnp.concatenate([high, low], axis=1), table)
+
+
+def lanes_result(product, count):
+    edge = product.shape[0] // count
     product = product[:, :lanes] + product[:, lanes:]
-    return [product[k * edge : (k + 1) * edge] for k in range(len(slabs))]
+    return [product[k * edge : (k + 1) * edge] for k in range(count)]
+
+
+def in_steps(count, *steps):
+    held = [{} for _ in steps]
+    for time in range(count + len(steps) - 1):
+        for n, step in enumerate(steps):
+            item = time - n
+            if 0 <= item < count:
+                given = (held[n - 1].pop(item),) if n else ()
+                held[n][item] = step(item, *given)
 
 
 def pair_kernel(
@@ -97,6 +110,7 @@
     left_fwd_ref, left_back_ref, right_fwd_ref, right_back_ref, near_ref, far_ref, work, back, result,
 ):
     group = lanes // math.gcd(lanes, grid_edge)
+    blocks = grid_edge // group
     tiles = group * grid_edge // lanes
     pitch = work.shape[0] // grid_edge
     planes = grid_edge // slots
@@ -115,7 +129,7 @@
         amount %= lanes
         return pltpu.roll(values, amount, 1) if amount else values
 
-    for block in range(grid_edge // group):
+    def first_lanes(block):
         home = tiles_of(home_ref, block)
         first = [a * b for a, b in zip(home, tiles_of(ahead_ref, block))]
         second = [turn(a * b, half) for a, b in zip(home, tiles_of(behind_ref, block))]
@@ -128,24 +142,44 @@
                 this_a = jnp.where(lane >= offset, this_a, first[tile + 1])
                 this_b = jnp.where(shifted >= offset, this_b, second[tile + 1])
             slabs.append(turn(jnp.where(in_first, this_a, this_b), -offset))
-        slabs = lanes_transform(slabs, right_fwd_ref[...])
-        slabs = rows_transform(left_fwd_ref[...], slabs)
+        return lanes_product(slabs, right_fwd_ref[...])
+
+    def first_rows(block, product):
+        return rows_products(left_fwd_ref[...], lanes_result(product, group))
+
+    def first_store(block, slabs):
         for k, slab in enumerate(slabs):
             work[pl.ds((block * group + k) * pitch, grid_edge), :] = slab
 
-    for block in range(grid_edge // group):
-        rows = [pl.ds(block * group + k, grid_edge, stride=pitch) for k in range(group)]
-        slabs = rows_transform(left_fwd_ref[...], [work[r, :] for r in rows])
-        slabs = [slab * kernel_ref[block * group + k] for k, slab in enumerate(slabs)]
-        slabs = rows_transform(left_back_ref[...], slabs)
-        for r, slab in zip(rows, slabs):
+    in_steps(blocks, first_lanes, first_rows, first_store)
+
+    together = 2
+
+    def rows_of(block):
+        return [pl.ds(block * together + k, grid_edge, stride=pitch) for k in range(together)]
+
+    def middle_forward(block):
+        return rows_products(left_fwd_ref[...], [work[r, :] for r in rows_of(block)])
+
+    def middle_back(block, slabs):
+        slabs = [slab * kernel_ref[block * together + k] for k, slab in enumerate(slabs)]
+        return rows_products(left_back_ref[...], slabs)
+
+    def middle_store(block, slabs):
+        for r, slab in zip(rows_of(block), slabs):
             back[r, :] = slab
 
-    for block in range(grid_edge // group):
+    in_steps(grid_edge // together, middle_forward, middle_back, middle_store)
+
+    def last_rows(block):
         slabs = [back[pl.ds((block * group + k) * pitch, grid_edge), :] for k in range(group)]
-        slabs = rows_transform(left_back_ref[...], slabs)
-        slabs = lanes_transform(slabs, right_back_ref[...])
-        slabs = [turn(slab, k * grid_edge) for k, slab in enumerate(slabs)]
+        return rows_products(left_back_ref[...], slabs)
+
+    def last_lanes(block, slabs):
+        return lanes_product(slabs, right_back_ref[...])
+
+    def last_store(block, product):
+        slabs = [turn(slab, k * grid_edge) for k, slab in enumerate(lanes_result(product, group))]
         ahead = tiles_of(ahead_ref, block)
         behind = tiles_of(behind_ref, block)
         for t in range(tiles):
@@ -159,6 +193,8 @@
             rows = pl.ds(block * tiles + t, planes, stride=row_tiles)
             for p in range(slots):
                 result[order_ref[p], rows, :] = total[p * planes : (p + 1) * planes]
+
+    in_steps(blocks, last_rows, last_lanes, last_store)
 
     for k in range(slots // 2):
         near_ref[k] = result[2 * k]
@@ -189,21 +225,16 @@
     )(order, home, ahead, behind, kernel, *(jnp.asarray(t) for t in tables))
 
 
-def offsets_of(cycle_size, groups):
-    bits = groups.bit_length() - 1
-    turned = [int(format(g, "b").zfill(bits)[::-1], 2) if bits else 0 for g in range(groups)]
-    ahead = [d if d else cycle_size // 2 for d in turned]
-    behind = [-d for d in turned]
-    return ahead, behind
-
-
-def fetch(block, offsets, cycle_size, groups):
-    route = []
-    for blk in range(cycle_size):
+def fetch(block, cycle_size, groups):
+    routes = ([], [])
+    for source in range(cycle_size):
         for g in range(groups):
-            if offsets[g] % cycle_size:
-                route.append(((blk + offsets[g]) % cycle_size * groups + g, blk * groups + g))
-    return lax.ppermute(block, ("blk", "off"), route)
+            near = sum(groups >> bit + 1 for bit in range(groups.bit_length() - 1) if g >> bit & 1)
+            for route, mask in zip(routes, (near, near ^ (groups + 1))):
+                route.append((source * groups + g, (source ^ mask) * groups + g))
+    near = lax.ppermute(block, ("blk", "off"), routes[0])
+    across = lax.ppermute(block, ("blk", "off"), routes[1])
+    return near, across
 
 
 def scattered_sum(near, far, groups):
@@ -223,19 +254,16 @@
     if cycle_size != 2 * groups or groups & (groups - 1) or groups < 2 or grid_edge > half:
         raise ValueError("unsupported mesh")
     me = lax.axis_index("off")
-    ahead_offsets, behind_offsets = offsets_of(cycle_size, groups)
-    behind = fetch(orbitals, behind_offsets, cycle_size, groups)
-    ahead = fetch(orbitals, ahead_offsets, cycle_size, groups)
-    behind = jnp.where(me == 0, orbitals, behind)
+    near, across = fetch(orbitals, cycle_size, groups)
     kernel = screened_kernel(grid_edge)
     order = jnp.arange(groups, dtype=jnp.int32) ^ me
     rows = []
     for i in range(band_count):
-        near = far = 0.0
+        own = rest = 0.0
         for j in range(band_count):
-            terms = pair_terms(order, orbitals[i], ahead[j], behind[j], kernel)
-            near, far = near + terms[0], far + terms[1]
-        rows.append(scattered_sum(near, far, groups))
+            terms = pair_terms(order, orbitals[i], near[j], across[j], kernel)
+            own, rest = own + terms[0], rest + terms[1]
+        rows.append(scattered_sum(own, rest, groups))
     return jnp.stack(rows).reshape(band_count, grid_edge // groups, plane_size)
 
 

time: 29.8 us -> 26.8 us (0.90)
  starting transfers between devices: 9.5 us -> 7.51 us
  Pallas kernels: 4.45 us -> 3.58 us
    ppermute x2, starting transfers between devices: 4.71 us -> 0.83 us  [scattered_sum(): arrived = lax.ppermute(far, 'off', [(g, g ^ bit) for g in range(groups)])]
    ppermute x2, starting transfers between devices: 4.8 us -> 6.69 us  [the longest x1 5.1 us: fetch(): across = lax.ppermute(block, ('blk', 'off'), routes[1])]
    ppermute x2, waiting for transfers between devices: 7.57 us -> 6.68 us  [the longest x1 6.68 us: fetch(): across = lax.ppermute(block, ('blk', 'off'), routes[1])]
    pallas_call x1, Pallas kernels: 4.45 us -> 3.58 us  [pair_terms(): pl.pallas_call(functools.partial(pair_kernel, grid_edge, slots), out_shap...]
    ppermute x2, waiting for transfers between devices: 5.06 us -> 5.87 us  [scattered_sum(): arrived = lax.ppermute(far, 'off', [(g, g ^ bit) for g in range(groups)])]
where the time goes in v4:
time: 26.8 us; the launch traced here: 26.7 us
  waiting for transfers between devices  12.6 us (47%)
  starting transfers between devices  7.51 us (28%)
  Pallas kernels  3.58 us (13%)
  other arithmetic  2.91 us (11%)
    ppermute x1, waiting for transfers between devices, fetch(): across = lax.ppermute(block, ('blk', 'off'), routes[1])  6.68 us
    ppermute x2, waiting for transfers between devices, scattered_sum(): arrived = lax.ppermute(far, 'off', [(g, g ^ bit) for g in range(groups)])  5.87 us
    ppermute x1, starting transfers between devices, fetch(): across = lax.ppermute(block, ('blk', 'off'), routes[1])  5.1 us
    pallas_call x1, Pallas kernels, pair_terms(): pl.pallas_call(functools.partial(pair_kernel, grid_edge, slots), out_shap...  3.58 us
    ppermute x1, starting transfers between devices, fetch(): near = lax.ppermute(block, ('blk', 'off'), routes[0])  1.58 us
    select_n x1, other arithmetic, screened_kernel(): jnp.where(squared == 0, jnp.float32(math.pi / screen_rate ** 2), screened)  1.41 us
    ppermute x2, starting transfers between devices, scattered_sum(): arrived = lax.ppermute(far, 'off', [(g, g ^ bit) for g in range(groups)])  0.83 us
    add x1, other arithmetic, screened_kernel(): squares[:, None, None] + squares[None, :, None]  0.8 us
  transfers between devices with their start and end apart: 4, of which 3 were waited for; matrix products, arithmetic and copies ran while one was open for 8% of the time, Pallas kernels for 0%

profile of v4, /device:TPU:0, one launch (start us, length us, event | category | flops | bytes accessed | tf_op | source)
XLA Modules:
  0.0 26.7 jit_solution(13378792510867137134)
XLA Ops:
  0.0 0.0 copy-start.1
  0.0 0.0 copy-start.2
  0.0 0.0 copy-start.3
  0.0 0.0 copy-start.4
  0.0 0.0 copy-start
  0.0 5.1 %collective-permute-start.1 = (bf16[1,48,2304]{2,1,0:T(8,128)(2,1)}, bf16[1,48,2304]{2,1,0:T(8,128)(2,1)S(1)}, u32[]{:S(2)}, u32[]{:S(2)}) collective-permute-start(bf16[1,48,2304]{2,1,0:T(8,128)(2,1)} %param.7), channel_id=1, source_target_pairs={{0,20},{1,29},{2,18},{3,27},{4,16},{5,25},{6,22},{7,31},{8,28},{9,... | collective-permute-start | bytes 663560 | tf_op jit(solution)/shard_map/ppermute | solution.py:236
  5.1 1.6 %collective-permute-start = (bf16[1,48,2304]{2,1,0:T(8,128)(2,1)}, bf16[1,48,2304]{2,1,0:T(8,128)(2,1)S(1)}, u32[]{:S(2)}, u32[]{:S(2)}) collective-permute-start(bf16[1,48,2304]{2,1,0:T(8,128)(2,1)} %param.7), channel_id=1, source_target_pairs={{0,0},{1,9},{2,6},{3,15},{4,4},{5,13},{6,2},{7,11},{8,8},{9,1},{10... | collective-permute-start | bytes 663560 | tf_op jit(solution)/shard_map/ppermute | solution.py:235
  6.7 0.8 %broadcast_add_fusion = s32[48,48]{1,0:T(8,128)S(1)} fusion(s32[48]{0:T(128)} %constant.29.clone), kind=kLoop, calls=%fused_computation.12 | loop fusion | flops 2304 | bytes 9408 | tf_op jit(solution)/shard_map/add | solution.py:58
  7.5 1.4 %fusion.kernel_ref = f32[48,48,128]{2,1,0:T(8,128)S(1)} fusion(s32[128]{0:T(128)} %constant.30.clone, s32[48,48]{1,0:T(8,128)S(1)} %broadcast_add_fusion), kind=kLoop, calls=%fused_computation.2 | loop fusion | flops 3244032 | bytes 1189376 | tf_op jit(solution)/shard_map/jit(_where)/select_n | solution.py:62
  8.9 6.7 %collective-permute-done.1 = bf16[1,48,2304]{2,1,0:T(8,128)(2,1)S(1)} collective-permute-done((bf16[1,48,2304]{2,1,0:T(8,128)(2,1)}, bf16[1,48,2304]{2,1,0:T(8,128)(2,1)S(1)}, u32[]{:S(2)}, u32[]{:S(2)}) %collective-permute-start.1) | collective-permute-done | bytes 221216 | tf_op jit(solution)/shard_map/ppermute | solution.py:236
  15.6 0.0 collective-permute-done
  15.6 0.0 copy-done.1
  15.6 0.0 copy-done.2
  15.6 0.0 copy-done.3
  15.6 0.0 copy-done.4
  15.6 0.0 copy-done
  15.6 3.6 %shard_map.73 = (f32[2,216,128]{2,1,0:T(8,128)S(1)}, f32[2,216,128]{2,1,0:T(8,128)S(1)}) custom-call(s32[4]{0:T(128)S(1)} %iota_xor_fusion.order_ref, bf16[48,2304]{1,0:T(8,128)(2,1)S(1)} %bitcast.4, bf16[48,2304]{1,0:T(8,128)(2,1)S(1)} %bitcast.6, bf16[48,2304]{1,0:T(8,128)(2,1)S(1)} %bitcast.5, f32[48,48,128]{2,1,0:T(8,128)S(1)} %fusion.kernel_ref, ...), custom_call_target="tpu_custom_call" | custom-call | flops 2000000000 | bytes 3000000 | tf_op jit(solution)/shard_map/pallas_call | solution.py:213
  19.2 0.1 collective-permute-start.2
  19.3 1.5 %collective-permute-done.2 = f32[2,216,128]{2,1,0:T(8,128)S(1)} collective-permute-done((f32[2,216,128]{2,1,0:T(8,128)S(1)}, f32[2,216,128]{2,1,0:T(8,128)S(1)}, u32[]{:S(2)}, u32[]{:S(2)}) %collective-permute-start.2) | collective-permute-done | bytes 221216 | tf_op jit(solution)/shard_map/ppermute | solution.py:243
  20.8 0.8 %collective-permute-start.3 = (f32[1,216,128]{2,1,0:T(8,128)S(1)}, f32[1,216,128]{2,1,0:T(8,128)S(1)}, u32[]{:S(2)}, u32[]{:S(2)}) collective-permute-start(f32[1,216,128]{2,1,0:T(8,128)S(1)} %slice.11), channel_id=1, source_target_pairs={{0,2},{1,3},{2,0},{3,1},{4,6},{5,7},{6,4},{7,5},{8,10},{9,11},{10,... | collective-permute-start | bytes 331784 | tf_op jit(solution)/shard_map/ppermute | solution.py:243
  21.6 4.4 %collective-permute-done.3 = f32[1,216,128]{2,1,0:T(8,128)S(1)} collective-permute-done((f32[1,216,128]{2,1,0:T(8,128)S(1)}, f32[1,216,128]{2,1,0:T(8,128)S(1)}, u32[]{:S(2)}, u32[]{:S(2)}) %collective-permute-start.3) | collective-permute-done | bytes 110624 | tf_op jit(solution)/shard_map/ppermute | solution.py:243
  26.0 0.7 %slice_add_fusion = f32[1,216,128]{2,1,0:T(8,128)} fusion(f32[1,216,128]{2,1,0:T(8,128)S(1)} %collective-permute-done.3, f32[2,216,128]{2,1,0:T(8,128)S(1)} %add.43), kind=kLoop, calls=%fused_computation.11 | loop fusion | flops 27648 | bytes 331776 | tf_op jit(solution)/shard_map/add | solution.py:244
  (3 shorter events, 0.0 us)
Async XLA Ops:
  0.0 15.6 %copy-start.1 = (bf16[256,256]{1,0:T(8,128)(2,1)S(1)}, bf16[256,256]{1,0:T(8,128)(2,1)}, u32[]{:S(2)}) copy-start(bf16[256,256]{1,0:T(8,128)(2,1)} %constant.34.clone.right_back_ref) | copy-start | bytes 393220
  0.0 15.6 %copy-start.2 = (bf16[256,256]{1,0:T(8,128)(2,1)S(1)}, bf16[256,256]{1,0:T(8,128)(2,1)}, u32[]{:S(2)}) copy-start(bf16[256,256]{1,0:T(8,128)(2,1)} %constant.33.clone.right_fwd_ref) | copy-start | bytes 393220
  0.0 15.6 %copy-start.3 = (bf16[48,144]{1,0:T(8,128)(2,1)S(1)}, bf16[48,144]{1,0:T(8,128)(2,1)}, u32[]{:S(2)}) copy-start(bf16[48,144]{1,0:T(8,128)(2,1)} %constant.32.clone.left_back_ref) | copy-start | bytes 41476
  0.0 15.6 %copy-start.4 = (bf16[48,144]{1,0:T(8,128)(2,1)S(1)}, bf16[48,144]{1,0:T(8,128)(2,1)}, u32[]{:S(2)}) copy-start(bf16[48,144]{1,0:T(8,128)(2,1)} %constant.31.clone.left_fwd_ref) | copy-start | bytes 41476
  0.0 15.6 %copy-start = (bf16[1,48,2304]{2,1,0:T(8,128)(2,1)S(1)}, bf16[1,48,2304]{2,1,0:T(8,128)(2,1)}, u32[]{:S(2)}) copy-start(bf16[1,48,2304]{2,1,0:T(8,128)(2,1)} %param.7) | copy-start | bytes 663556
  0.0 15.6 %collective-permute-start.1 = (bf16[1,48,2304]{2,1,0:T(8,128)(2,1)}, bf16[1,48,2304]{2,1,0:T(8,128)(2,1)S(1)}, u32[]{:S(2)}, u32[]{:S(2)}) collective-permute-start(bf16[1,48,2304]{2,1,0:T(8,128)(2,1)} %param.7), channel_id=1, source_target_pairs={{0,20},{1,29},{2,18},{3,27},{4,16},{5,25},{6,22},{7,31},{8,28},{9,... | collective-permute-start | bytes 663560 | tf_op jit(solution)/shard_map/ppermute | solution.py:236
  5.1 10.5 %collective-permute-start = (bf16[1,48,2304]{2,1,0:T(8,128)(2,1)}, bf16[1,48,2304]{2,1,0:T(8,128)(2,1)S(1)}, u32[]{:S(2)}, u32[]{:S(2)}) collective-permute-start(bf16[1,48,2304]{2,1,0:T(8,128)(2,1)} %param.7), channel_id=1, source_target_pairs={{0,0},{1,9},{2,6},{3,15},{4,4},{5,13},{6,2},{7,11},{8,8},{9,1},{10... | collective-permute-start | bytes 663560 | tf_op jit(solution)/shard_map/ppermute | solution.py:235
  19.2 1.5 %collective-permute-start.2 = (f32[2,216,128]{2,1,0:T(8,128)S(1)}, f32[2,216,128]{2,1,0:T(8,128)S(1)}, u32[]{:S(2)}, u32[]{:S(2)}) collective-permute-start(f32[2,216,128]{2,1,0:T(8,128)S(1)} %get-tuple-element.8), channel_id=1, source_target_pairs={{0,1},{1,0},{2,3},{3,2},{4,5},{5,4},{6,7},{7,6},{8,9},{9,8},{10,11... | collective-permute-start | bytes 663560 | tf_op jit(solution)/shard_map/ppermute | solution.py:243
  20.8 5.2 %collective-permute-start.3 = (f32[1,216,128]{2,1,0:T(8,128)S(1)}, f32[1,216,128]{2,1,0:T(8,128)S(1)}, u32[]{:S(2)}, u32[]{:S(2)}) collective-permute-start(f32[1,216,128]{2,1,0:T(8,128)S(1)} %slice.11), channel_id=1, source_target_pairs={{0,2},{1,3},{2,0},{3,1},{4,6},{5,7},{6,4},{7,5},{8,10},{9,11},{10,... | collective-permute-start | bytes 331784 | tf_op jit(solution)/shard_map/ppermute | solution.py:243
